TPU v7x, 32 devices: a whole 2x2x4 slice. The times are simulated.
32 devices in a mesh: band: 8 (over y, x, core), pw: 4 (over z).
Axes of the slice: x: 2, y: 2, z: 4, core: 2. Of those that a mesh axis runs over, the one named last changes fastest.
Arguments:
- pair_density: bfloat16 [40, 128, 9216], P('band', None, 'pw'), may hold values from -6 to 6
- eigvecs: bfloat16 [2944, 9216], P('band', 'pw'), may hold values from -0.0625 to 0.0625
- screening: bfloat16 [2944, 2944], P('pw'), may hold values from -0.00048828125 to 0.00048828125
- occupation: float32 [16], replicated, may hold values from 0 to 1
- window_start: int32 [40], P('band'), may hold values from 0 to 511, as said below
- window_len: int32 [40], P('band'), may hold values from 1 to 128, as said below
- slot_band: int32 [40], P('band'), may hold values from -1 to 15, as said below
Outputs:
- sigma: float32 [512, 512], P(('band', 'pw'))
Inputs may be any that keep to these rules, and one draw needn't show every extreme that they name: window_start + window_len <= 512 for every slot. `window_len`: some slot has a window of 128 bands. On each index of band the live slots (slot_band >= 0) come first among its 5 slots; each index holds 3 to 5 live slots, and the counts of index i and index i + 8 / 2 add up to 8.
All inputs are finite; a program needn't handle non-finite values.
Results may differ from a plain program's by a relative error of at most 0.0049.
Values may be sent and summed in bfloat16 or wider, within the bound.
A program may use at most 128 MiB of HBM per device.

v0:
```python
import functools

import jax
import jax.numpy as jnp
from jax import lax
from jax.experimental import pallas as pl
from jax.experimental.pallas import tpu as pltpu
from jax.sharding import PartitionSpec as P

NB_SIGMA = 512


def ring_per_device(pair_density, eigvecs, screening, occupation, window_start, window_len, slot_band):
    capacity, block, plane_rows = pair_density.shape
    density, starts, lengths, band_ids = (pair_density, window_start, window_len, slot_band)
    slots = density.shape[0]
    flat = density.reshape(slots * block, plane_rows)
    partial_proj = lax.dot_general(
        flat,
        lax.all_gather(eigvecs, "band", axis=0, tiled=True),
        (((1,), (1,)), ((), ())),
        preferred_element_type=jnp.float32,
    )
    row_ids = jnp.arange(block, dtype=jnp.int32)
    keep_rows = ((row_ids[None, :] < lengths[:, None]) & (band_ids[:, None] >= 0)).astype(
        jnp.float32
    )
    masked = partial_proj * keep_rows.reshape(slots * block, 1)
    projected = lax.psum(masked, "pw").astype(jnp.bfloat16)
    width = screening.shape[0]
    own_cols = lax.dynamic_slice_in_dim(projected, lax.axis_index("pw") * width, width, 1)
    screened = lax.dot_general(
        projected, screening, (((1,), (1,)), ((), ())), preferred_element_type=jnp.float32
    ).astype(jnp.bfloat16)
    block_sigma = lax.dot_general(
        screened.reshape(slots, block, width),
        own_cols.reshape(slots, block, width),
        (((2,), (2,)), ((0,), (0,))),
        preferred_element_type=jnp.float32,
    )
    band_list = jnp.arange(occupation.shape[0], dtype=jnp.int32)
    weights = 0.5 - jnp.sum(
        jnp.where(band_list[None, :] == band_ids[:, None], occupation[None, :], 0.0), axis=1
    )
    totals = jnp.zeros((NB_SIGMA + block, NB_SIGMA + block), jnp.float32)
    for index in range(slots):
        first = starts[index]
        previous = lax.dynamic_slice(totals, (first, first), (block, block))
        totals = lax.dynamic_update_slice(
            totals, previous + weights[index] * block_sigma[index], (first, first)
        )
    sigma_part = totals[:NB_SIGMA, :NB_SIGMA]
    by_band = lax.psum_scatter(sigma_part, "band", scatter_dimension=0, tiled=True)
    return lax.psum_scatter(by_band, "pw", scatter_dimension=0, tiled=True)


def flip(index, relation):
    total = 0
    for place in (4, 2, 1):
        bit = lax.rem(index // place, 2)
        other = lax.rem(relation // place, 2)
        total = total + place * (bit + other - 2 * bit * other)
    return total


def split(value):
    top = value.astype(jnp.bfloat16)
    return top, (value - top.astype(jnp.float32)).astype(jnp.bfloat16)


def fused_kernel(
    density_ref, eig_ref, screen_ref, meta_ref, out_ref,
    density, extra, extra_meta, meta, eig, screen, part, sent, own, landed, proj, acc,
    place, high, low, sigma, band_sum, sigma_in, band_in,
    load_sem, extra_send, extra_recv, half_send, half_recv, eig_send, eig_recv, red_send, red_recv, up_send, up_recv, down_send, down_recv,
    sig_send, sig_recv, fin_send, fin_recv,
):
    mesh_id = pl.DeviceIdType.MESH
    band, z = lax.axis_index("band"), lax.axis_index("pw")
    n_rel, depth, _ = eig.shape
    n_z = landed.shape[1] + 1
    rows = own.shape[1]
    slots, block = n_z, rows
    last = slots * block

    barrier = pltpu.get_barrier_semaphore()
    for rel in range(1, n_rel):
        pl.semaphore_signal(barrier, inc=1, device_id=(flip(band, rel), z), device_id_type=mesh_id)
    for k in range(1, n_z):
        pl.semaphore_signal(
            barrier, inc=1, device_id=(band, lax.rem(z + k, n_z)), device_id_type=mesh_id
        )
    loads = [
        pltpu.make_async_copy(density_ref.at[pl.ds(0, last)], density, load_sem.at[0]),
        pltpu.make_async_copy(eig_ref, eig.at[0], load_sem.at[1]),
    ]
    for load in loads:
        load.start()
    pl.semaphore_wait(barrier, n_rel - 1 + n_z - 1)

    middle = -(-depth // 32) * 16
    halves = (pl.ds(0, middle), pl.ds(middle, depth - middle))

    def half_copy(rel, half):
        return pltpu.make_async_remote_copy(
            src_ref=eig_ref.at[halves[half]], dst_ref=eig.at[rel, halves[half]],
            send_sem=half_send.at[half, rel], recv_sem=half_recv.at[half, rel],
            device_id=(flip(band, rel), z), device_id_type=mesh_id,
        )

    def corner_copy(half):
        via = (2, 4)[half]
        return pltpu.make_async_remote_copy(
            src_ref=eig.at[via, halves[half]], dst_ref=eig.at[6, halves[half]],
            send_sem=half_send.at[half, 6], recv_sem=half_recv.at[half, 6],
            device_id=(flip(band, 6 - via), z), device_id_type=mesh_id,
        )

    def eig_copy(rel):
        return pltpu.make_async_remote_copy(
            src_ref=eig_ref, dst_ref=eig.at[rel], send_sem=eig_send.at[rel],
            recv_sem=eig_recv.at[rel], device_id=(flip(band, rel), z), device_id_type=mesh_id,
        )

    def forward_copy(rel):
        return pltpu.make_async_remote_copy(
            src_ref=eig.at[rel], dst_ref=eig.at[rel + 1], send_sem=eig_send.at[rel + 1],
            recv_sem=eig_recv.at[rel + 1], device_id=(flip(band, 1), z), device_id_type=mesh_id,
        )

    partner = (flip(band, n_rel // 2), z)
    swaps = [
        pltpu.make_async_remote_copy(
            src_ref=source, dst_ref=target, send_sem=extra_send.at[index],
            recv_sem=extra_recv.at[index], device_id=partner, device_id_type=mesh_id,
        )
        for index, (source, target) in enumerate(
            [(density_ref.at[pl.ds(last, block)], extra), (meta_ref.at[slots], extra_meta)]
        )
    ]
    for swap in swaps:
        swap.start()
    for rel, half in ((2, 0), (4, 1), (2, 1), (4, 0)):
        half_copy(rel, half).start()
    eig_copy(1).start()
    def red_copy(rel, k):
        target = lax.rem(z + k, n_z)
        return pltpu.make_async_remote_copy(
            src_ref=sent.at[rel, target], dst_ref=landed.at[rel, k - 1],
            send_sem=red_send.at[rel, k - 1], recv_sem=red_recv.at[rel, k - 1],
            device_id=(band, target), device_id_type=mesh_id,
        )

    def up_copy(rel, hop):
        source = lax.rem(z - hop + n_z, n_z)
        return pltpu.make_async_remote_copy(
            src_ref=proj.at[rel, source], dst_ref=proj.at[rel, source],
            send_sem=up_send.at[rel, hop], recv_sem=up_recv.at[rel, hop],
            device_id=(band, lax.rem(z + 1, n_z)), device_id_type=mesh_id,
        )

    def down_copy(rel, hop):
        source = lax.rem(z + hop, n_z)
        return pltpu.make_async_remote_copy(
            src_ref=proj.at[rel, source], dst_ref=proj.at[rel, source],
            send_sem=down_send.at[rel, hop], recv_sem=down_recv.at[rel, hop],
            device_id=(band, lax.rem(z + n_z - 1, n_z)), device_id_type=mesh_id,
        )

    def landing(rel, hop, up):
        source = lax.rem(z - hop - 1 + 2 * n_z, n_z) if up else lax.rem(z + hop + 1, n_z)
        return pltpu.make_async_remote_copy(
            src_ref=proj.at[rel, source], dst_ref=proj.at[rel, source],
            send_sem=(up_send if up else down_send).at[rel, hop],
            recv_sem=(up_recv if up else down_recv).at[rel, hop],
            device_id=(band, lax.rem(z + 1, n_z)), device_id_type=mesh_id,
        )

    def pass_on(rel, hop):
        @pl.when((z - hop >= 0) & (z + 1 < n_z))
        def _():
            up_copy(rel, hop).start()

        @pl.when((z + hop < n_z) & (z >= 1))
        def _():
            down_copy(rel, hop).start()

    def take(rel, hop):
        @pl.when(z - hop - 1 >= 0)
        def _():
            landing(rel, hop, True).wait_recv()

        @pl.when(z + hop + 1 < n_z)
        def _():
            landing(rel, hop, False).wait_recv()

    def multiply(rel, first, stop):
        result = lax.dot_general(
            density[first * block : stop * block], eig[rel], (((1,), (1,)), ((), ())),
            preferred_element_type=jnp.float32,
        ).reshape(stop - first, block, depth)
        part[first:stop] = result
        sent[rel, first:stop] = result.astype(jnp.bfloat16)

        @pl.when((z >= first) & (z < stop))
        def _():
            own[rel] = part[z]

        for k in (2, 1, 3):
            target = lax.rem(z + k, n_z)

            @pl.when((target >= first) & (target < stop))
            def _():
                red_copy(rel, k).start()

    def project(rel):
        @pl.when(lax.rem(rel, 2) == 1)
        def _():
            eig_copy(rel).wait_recv()

        @pl.when(rel == 2)
        def _():
            half_copy(2, 0).wait_recv()
            corner_copy(0).start()
            half_copy(4, 1).wait_recv()
            corner_copy(1).start()
            half_copy(2, 1).wait_recv()

        @pl.when(rel == 4)
        def _():
            half_copy(4, 0).wait_recv()

        @pl.when(rel == 6)
        def _():
            corner_copy(0).wait_recv()
            corner_copy(1).wait_recv()

        @pl.when((rel >= 2) & (lax.rem(rel, 2) == 0))
        def _():
            forward_copy(rel).start()

        @pl.when(rel == 0)
        def _():
            for swap in swaps:
                swap.wait_recv()
            taken = meta_ref[slots - 1, 0:1, 0:1] > 0.0
            for slot in range(slots - 1):
                meta[slot] = meta_ref[slot]
            meta[slots - 1] = jnp.where(taken, meta_ref[slots - 1], extra_meta[...])
            tail = density[last - block :]
            density[last - block :] = jnp.where(taken, tail, extra[...])
            multiply(rel, slots - 1, slots)

        @pl.when(rel > 0)
        def _():
            multiply(rel, 0, slots)

    def reduce(rel):
        for k in range(1, n_z):
            red_copy(rel, k).wait_recv()
        total = own[rel]
        for k in range(1, n_z):
            total = total + landed[rel, k - 1].astype(jnp.float32)
        row_ids = lax.broadcasted_iota(jnp.int32, total.shape, 0).astype(jnp.float32)
        keep = jnp.where(row_ids < meta[z, 0:1, 0:1], 1.0, 0.0)
        proj[rel, z] = (total * keep).astype(jnp.bfloat16)
        pass_on(rel, 0)

    def screen_step(rel):
        take(rel, n_z - 2)
        whole = proj[rel].reshape(n_z * rows, depth)
        at = flip(band, rel)
        for half in range(2):
            acc[half] += lax.dot_general(
                whole, screen[at, half * depth : (half + 1) * depth], (((1,), (1,)), ((), ())),
                preferred_element_type=jnp.float32,
            )

    def step(t, carry):
        @pl.when(t < n_rel)
        def _():
            project(t)

        @pl.when((t >= 1) & (t < n_rel + 1))
        def _():
            reduce(t - 1)

        for hop in range(n_z - 2):
            @pl.when((t >= 2 + hop) & (t < n_rel + 2 + hop))
            def _():
                take(t - 2 - hop, hop)
                pass_on(t - 2 - hop, hop + 1)

        @pl.when(t >= n_z)
        def _():
            screen_step(t - n_z)

        return carry

    for load in loads:
        load.wait()
    multiply(0, 0, slots - 1)
    for index in range(n_rel):
        screen[index] = screen_ref[:, index * depth : (index + 1) * depth]
    acc[...] = jnp.zeros_like(acc)
    lax.fori_loop(0, n_rel + n_z, step, 0)

    screened = acc[...].astype(jnp.bfloat16)
    pairs = [proj[flip(band, 2 * z + half)].reshape(n_z * rows, depth) for half in range(2)]
    for slot in range(slots):
        here = slice(slot * block, (slot + 1) * block)
        total = 0.0
        for half in range(2):
            total = total + lax.dot_general(
                screened[half, here], pairs[half][here], (((1,), (1,)), ((), ())),
                preferred_element_type=jnp.float32,
            )
        total = total * meta[slot, 1:2]
        bands = lax.broadcasted_iota(jnp.int32, (place.shape[0], block), 0).astype(jnp.float32)
        window = lax.broadcasted_iota(jnp.int32, (place.shape[0], block), 1).astype(jnp.float32)
        window = window + meta[slot, 2:3]
        onehot = jnp.where(bands == window, 1.0, 0.0).astype(jnp.bfloat16)
        place[:, here] = onehot
        spread = 0.0
        for piece in split(total):
            spread = spread + jnp.dot(onehot, piece, preferred_element_type=jnp.float32)
        high[:, here], low[:, here] = split(spread)

    whole = 0.0
    for piece in (high, low):
        whole = whole + lax.dot_general(
            piece[...], place[...], (((1,), (1,)), ((), ())), preferred_element_type=jnp.float32
        )
    sigma[...] = whole.reshape(sigma.shape)

    def sigma_copy(rel):
        target = flip(band, rel)
        return pltpu.make_async_remote_copy(
            src_ref=sigma.at[target], dst_ref=sigma_in.at[rel - 1],
            send_sem=sig_send.at[rel - 1], recv_sem=sig_recv.at[rel - 1],
            device_id=(target, z), device_id_type=mesh_id,
        )

    def final_copy(k):
        target = lax.rem(z + k, n_z)
        return pltpu.make_async_remote_copy(
            src_ref=band_sum.at[target], dst_ref=band_in.at[k - 1],
            send_sem=fin_send.at[k - 1], recv_sem=fin_recv.at[k - 1],
            device_id=(band, target), device_id_type=mesh_id,
        )

    for rel in (6, 7, 2, 4, 3, 5, 1):
        sigma_copy(rel).start()
    total = sigma[band]
    for rel in range(1, n_rel):
        sigma_copy(rel).wait_recv()
        total = total + sigma_in[rel - 1]
    band_sum[...] = total.reshape(band_sum.shape)
    for k in (2, 1, 3):
        final_copy(k).start()
    total = band_sum[z]
    for k in range(1, n_z):
        final_copy(k).wait_recv()
        total = total + band_in[k - 1]
    out_ref[...] = total

    for rel in range(1, n_rel):
        sigma_copy(rel).wait_send()
    for k in range(1, n_z):
        final_copy(k).wait_send()

    for swap in swaps:
        swap.wait_send()
    eig_copy(1).wait_send()
    for half in range(2):
        corner_copy(half).wait_send()
        for rel in (2, 4):
            half_copy(rel, half).wait_send()
    for rel in (2, 4, 6):
        forward_copy(rel).wait_send()

    def drain(rel, carry):
        for k in range(1, n_z):
            red_copy(rel, k).wait_send()
        for hop in range(n_z - 1):
            @pl.when((z - hop >= 0) & (z + 1 < n_z))
            def _():
                up_copy(rel, hop).wait_send()

            @pl.when((z + hop < n_z) & (z >= 1))
            def _():
                down_copy(rel, hop).wait_send()
        return carry

    lax.fori_loop(0, n_rel, drain, 0)


def per_device(
    n_z, n_rel, pair_density, eigvecs, screening, occupation, window_start, window_len, slot_band
):
    capacity, block, plane_rows = pair_density.shape
    depth, width = eigvecs.shape[0], screening.shape[0]
    slots, rows = n_z, block
    kept = jnp.where(slot_band >= 0, window_len, 0).astype(jnp.float32)
    band_list = jnp.arange(occupation.shape[0], dtype=jnp.int32)
    weights = 0.5 - jnp.sum(
        jnp.where(band_list[None, :] == slot_band[:, None], occupation[None, :], 0.0), axis=1
    )
    fields = jnp.stack([kept, weights, window_start.astype(jnp.float32)], axis=1)
    meta = jnp.broadcast_to(jnp.pad(fields, ((0, 0), (0, 5)))[:, :, None], (capacity, 8, block))
    dma = pltpu.SemaphoreType.DMA
    vmem = pl.BlockSpec(memory_space=pltpu.VMEM)
    strip = NB_SIGMA // (n_rel * n_z)
    return pl.pallas_call(
        fused_kernel,
        out_shape=jax.ShapeDtypeStruct((strip, NB_SIGMA), jnp.float32),
        in_specs=[
            pl.BlockSpec(memory_space=pl.ANY), pl.BlockSpec(memory_space=pl.ANY), vmem, vmem,
        ],
        out_specs=vmem,
        scratch_shapes=[
            pltpu.VMEM((slots * block, plane_rows), jnp.bfloat16),
            pltpu.VMEM((block, plane_rows), jnp.bfloat16),
            pltpu.VMEM((8, block), jnp.float32),
            pltpu.VMEM((slots, 8, block), jnp.float32),
            pltpu.VMEM((n_rel, depth, plane_rows), jnp.bfloat16),
            pltpu.VMEM((n_rel, width, depth), jnp.bfloat16),
            pltpu.VMEM((n_z, rows, depth), jnp.float32),
            pltpu.VMEM((n_rel, n_z, rows, depth), jnp.bfloat16),
            pltpu.VMEM((n_rel, rows, depth), jnp.float32),
            pltpu.VMEM((n_rel, n_z - 1, rows, depth), jnp.bfloat16),
            pltpu.VMEM((n_rel, n_z, rows, depth), jnp.bfloat16),
            pltpu.VMEM((2, slots * block, depth), jnp.float32),
            pltpu.VMEM((NB_SIGMA, slots * block), jnp.bfloat16),
            pltpu.VMEM((NB_SIGMA, slots * block), jnp.bfloat16),
            pltpu.VMEM((NB_SIGMA, slots * block), jnp.bfloat16),
            pltpu.VMEM((n_rel, n_z * strip, NB_SIGMA), jnp.float32),
            pltpu.VMEM((n_z, strip, NB_SIGMA), jnp.float32),
            pltpu.VMEM((n_rel - 1, n_z * strip, NB_SIGMA), jnp.float32),
            pltpu.VMEM((n_z - 1, strip, NB_SIGMA), jnp.float32),
            dma((2,)),
            dma((2,)),
            dma((2,)),
            dma((2, n_rel)),
            dma((2, n_rel)),
            dma((n_rel,)),
            dma((n_rel,)),
            dma((n_rel, n_z - 1)),
            dma((n_rel, n_z - 1)),
            dma((n_rel, n_z - 1)),
            dma((n_rel, n_z - 1)),
            dma((n_rel, n_z - 1)),
            dma((n_rel, n_z - 1)),
            dma((n_rel - 1,)),
            dma((n_rel - 1,)),
            dma((n_z - 1,)),
            dma((n_z - 1,)),
        ],
        compiler_params=pltpu.CompilerParams(
            collective_id=0, has_side_effects=True, vmem_limit_bytes=60 * 2**20
        ),
    )(
        pair_density.reshape(capacity * block, plane_rows),
        eigvecs,
        screening,
        meta,
    )


def solution(mesh):
    n_band, n_z = mesh.shape["band"], mesh.shape["pw"]
    body = ring_per_device
    if n_band == 8 and n_z == 4:
        body = functools.partial(per_device, n_z, n_band)
    return jax.shard_map(
        body,
        mesh=mesh,
        in_specs=(
            P("band", None, "pw"),
            P("band", "pw"),
            P("pw", None),
            P(),
            P("band"),
            P("band"),
            P("band"),
        ),
        out_specs=P(("band", "pw"), None),
        check_vma=False,
    )
```

profile of v0, /device:TPU:1, one launch (start us, length us, event | category | flops | bytes accessed | tf_op | source)
XLA Modules:
  0.0 158.7 jit_solution(1294756576149673188)
XLA Ops:
  0.0 0.9 select_reduce_fusion
  0.9 0.7 fusion.1
  1.6 0.1 copy.10
  1.7 0.7 broadcast_in_dim.25.meta_ref
  2.4 155.0 %shard_map.73 = f32[16,512]{1,0:T(8,128)} custom-call(bf16[640,2304]{1,0:T(8,128)(2,1)} %bitcast.7, bf16[368,2304]{1,0:T(8,128)(2,1)} %eig_ref.1, bf16[736,2944]{1,0:T(8,128)(2,1)} %screen_ref.1, f32[5,8,128]{2,1,0:T(8,128)} %broadcast_in_dim.25.meta_ref), custom_call_target="tpu_custom_call" | custom-call | tf_op jit(solution)/shard_map/pallas_call | solution.py:414
  157.3 1.4 copy.12
  (3 shorter events, 0.0 us)
where the time goes:
time: 159 us
  Pallas kernels  155 us (97%)
  local copies, waits for them, and re-layouts  2.16 us (1%)
    pallas_call x1, Pallas kernels, per_device(): pl.pallas_call(fused_kernel, out_shape=jax.ShapeDtypeStruct((strip, NB_SI...  155 us

commit v1 on v0

v1 whole, which is shorter than its diff:
```python
import functools

import jax
import jax.numpy as jnp
from jax import lax
from jax.experimental import pallas as pl
from jax.experimental.pallas import tpu as pltpu
from jax.sharding import PartitionSpec as P

NB_SIGMA = 512


def ring_per_device(pair_density, eigvecs, screening, occupation, window_start, window_len, slot_band):
    capacity, block, plane_rows = pair_density.shape
    density, starts, lengths, band_ids = (pair_density, window_start, window_len, slot_band)
    slots = density.shape[0]
    flat = density.reshape(slots * block, plane_rows)
    partial_proj = lax.dot_general(
        flat,
        lax.all_gather(eigvecs, "band", axis=0, tiled=True),
        (((1,), (1,)), ((), ())),
        preferred_element_type=jnp.float32,
    )
    row_ids = jnp.arange(block, dtype=jnp.int32)
    keep_rows = ((row_ids[None, :] < lengths[:, None]) & (band_ids[:, None] >= 0)).astype(
        jnp.float32
    )
    masked = partial_proj * keep_rows.reshape(slots * block, 1)
    projected = lax.psum(masked, "pw").astype(jnp.bfloat16)
    width = screening.shape[0]
    own_cols = lax.dynamic_slice_in_dim(projected, lax.axis_index("pw") * width, width, 1)
    screened = lax.dot_general(
        projected, screening, (((1,), (1,)), ((), ())), preferred_element_type=jnp.float32
    ).astype(jnp.bfloat16)
    block_sigma = lax.dot_general(
        screened.reshape(slots, block, width),
        own_cols.reshape(slots, block, width),
        (((2,), (2,)), ((0,), (0,))),
        preferred_element_type=jnp.float32,
    )
    band_list = jnp.arange(occupation.shape[0], dtype=jnp.int32)
    weights = 0.5 - jnp.sum(
        jnp.where(band_list[None, :] == band_ids[:, None], occupation[None, :], 0.0), axis=1
    )
    totals = jnp.zeros((NB_SIGMA + block, NB_SIGMA + block), jnp.float32)
    for index in range(slots):
        first = starts[index]
        previous = lax.dynamic_slice(totals, (first, first), (block, block))
        totals = lax.dynamic_update_slice(
            totals, previous + weights[index] * block_sigma[index], (first, first)
        )
    sigma_part = totals[:NB_SIGMA, :NB_SIGMA]
    by_band = lax.psum_scatter(sigma_part, "band", scatter_dimension=0, tiled=True)
    return lax.psum_scatter(by_band, "pw", scatter_dimension=0, tiled=True)


def flip(index, relation):
    total = 0
    for place in (4, 2, 1):
        bit = lax.rem(index // place, 2)
        other = lax.rem(relation // place, 2)
        total = total + place * (bit + other - 2 * bit * other)
    return total


def split(value):
    top = value.astype(jnp.bfloat16)
    return top, (value - top.astype(jnp.float32)).astype(jnp.bfloat16)


N_QUARTER = 4
EARLY, PATCH, FULL = 2 * N_QUARTER, 2, 6 * N_QUARTER
TICKS = EARLY + PATCH + FULL
LAG_SUM, LAG_TOTAL, LAG_SCREEN = 2, 5, 8


def piece_of(order):
    pair, core = lax.div(order, 2), lax.rem(order, 2)
    late = lax.div(pair, 8)
    side = lax.rem(pair + 1, 2) + lax.div(pair, 7) - 1 + lax.div(pair + 7, 8)
    near = lax.rem(lax.div(pair + 1, 2), 4)
    rest = pair - 8 * late
    corner = lax.rem(rest + 1, 3) + 2 * lax.div(rest, 3)
    relation = (1 - late) * (2 + 2 * side) + late * 6 + core
    return relation, (1 - late) * near + late * corner


def fused_kernel(
    density_ref, eig_ref, screen_ref, start_ref, len_ref, slot_ref, occ_ref, out_ref,
    density, extra, extra_out, extra_meta, meta, keep, eig, stage, screen, part, sent, from_edge, from_mid,
    proj, acc, place, high, low, sig_out, sig_own, sig_in, xy_in, band_sum, fin_in,
    load_sem, swap_send, swap_recv, eig_send, eig_recv, z_send, z_recv, sig_send, sig_recv, xy_send, xy_recv,
    fin_send, fin_recv,
):
    mesh_id = pl.DeviceIdType.MESH
    band, z = lax.axis_index("band"), lax.axis_index("pw")
    n_rel, padded, _ = eig.shape
    depth = eig_ref.shape[0]
    piece = padded // N_QUARTER
    short = depth - (N_QUARTER - 1) * piece
    block = extra.shape[0]
    cols = density.shape[0]
    slots = cols // block
    most = cols - block
    n_z = fin_in.shape[0] + 1
    mate, across = z + 1 - 2 * lax.rem(z, 2), n_z - 1 - z
    inner = (z == 1) | (z == 2)
    edge = (z == 0) | (z == n_z - 1)
    whole_rows = pl.ds(0, depth)

    loads = [
        pltpu.make_async_copy(eig_ref, eig.at[0, whole_rows], load_sem.at[0]),
        pltpu.make_async_copy(density_ref.at[pl.ds(0, cols)], density, load_sem.at[1]),
        pltpu.make_async_copy(screen_ref, stage, load_sem.at[2]),
    ]
    for load in loads:
        load.start()

    def fields(slot):
        live = slot_ref[slot] >= 0
        kept = jnp.where(live, len_ref[slot], 0).astype(jnp.float32)
        weight = jnp.where(live, 0.5 - occ_ref[jnp.maximum(slot_ref[slot], 0)], 0.5)
        first = start_ref[slot].astype(jnp.float32)
        row = lax.broadcasted_iota(jnp.int32, (8, block), 0)
        return jnp.where(row == 0, kept, jnp.where(row == 1, weight, first))

    extra_out[...] = fields(slots)
    for slot in range(slots):
        meta[slot] = fields(slot)

    barrier = pltpu.get_barrier_semaphore()
    for rel in range(1, n_rel):
        pl.semaphore_signal(barrier, inc=1, device_id=(flip(band, rel), z), device_id_type=mesh_id)
    for k in range(1, n_z):
        pl.semaphore_signal(
            barrier, inc=1, device_id=(band, lax.rem(z + k, n_z)), device_id_type=mesh_id
        )
    tail = pl.ds(depth, padded - depth)
    for rel in range(n_rel):
        eig[rel, tail] = jnp.zeros((padded - depth, eig.shape[2]), eig.dtype)
        for buffer in (from_edge, from_mid, proj):
            buffer[rel, tail] = jnp.zeros((padded - depth, cols), buffer.dtype)
    acc[...] = jnp.zeros_like(acc)
    lanes = lax.broadcasted_iota(jnp.int32, (8, block), 1).astype(jnp.float32)
    for slot in range(slots):
        keep[:, slot * block : (slot + 1) * block] = jnp.where(lanes < meta[slot, 0:1], 1.0, 0.0)
    pl.semaphore_wait(barrier, n_rel - 1 + n_z - 1)

    def remote(source, target, send, recv, device):
        return pltpu.make_async_remote_copy(
            src_ref=source, dst_ref=target, send_sem=send, recv_sem=recv,
            device_id=device, device_id_type=mesh_id,
        )

    def rows_at(quarter, rows):
        if isinstance(quarter, int):
            return pl.ds(quarter * piece, rows)
        return pl.ds(pl.multiple_of(quarter * piece, 16), rows)

    def each(quarter, act):
        if isinstance(quarter, int):
            act(rows_at(quarter, piece if quarter < N_QUARTER - 1 else short))
            return

        @pl.when(quarter < N_QUARTER - 1)
        def _():
            act(rows_at(quarter, piece))

        @pl.when(quarter == N_QUARTER - 1)
        def _():
            act(rows_at(quarter, short))

    def own_copy(rel, quarter, rows):
        return remote(
            eig_ref.at[rows], eig.at[rel, rows], eig_send.at[rel, quarter],
            eig_recv.at[rel, quarter], (flip(band, rel), z),
        )

    def forward_copy(rel, quarter, rows):
        return remote(
            eig.at[rel, rows], eig.at[rel + 1, rows], eig_send.at[rel + 1, quarter],
            eig_recv.at[rel + 1, quarter], (flip(band, 1), z),
        )

    def corner_copy(via, quarter, rows):
        return remote(
            eig.at[via, rows], eig.at[6, rows], eig_send.at[6, quarter],
            eig_recv.at[6, quarter], (flip(band, 6 - via), z),
        )

    def landed(rel, quarter, rows):
        return remote(
            eig.at[rel, rows], eig.at[rel, rows], eig_send.at[rel, quarter],
            eig_recv.at[rel, quarter], (flip(band, 1), z),
        )

    def z_copy(kind, rel, quarter, rows, columns):
        source, target = ((sent, from_edge), (sent, from_mid), (proj, proj))[kind]
        return remote(
            source.at[rel, rows, columns], target.at[rel, rows, columns],
            z_send.at[kind, rel, quarter], z_recv.at[kind, rel, quarter],
            (band, across if kind == 1 else mate),
        )

    swaps = [
        remote(source, target, swap_send.at[index], swap_recv.at[index], (flip(band, 4), z))
        for index, (source, target) in enumerate(
            [(density_ref.at[pl.ds(cols, block)], extra), (extra_out, extra_meta)]
        )
    ]
    for swap in swaps:
        swap.start()
    for index in range(N_QUARTER):
        for rel, quarter in ((1, index), (2, index), (4, (index + 1) % N_QUARTER)):
            each(quarter, lambda rows: own_copy(rel, quarter, rows).start())

    first_cols, last_cols, all_cols = pl.ds(0, most), pl.ds(most, block), pl.ds(0, cols)

    def items(index, whole, act):
        @pl.when((index >= 0) & (index < EARLY))
        def _():
            rel, quarter = lax.rem(index, 2), lax.div(index, 2)
            act(rel, quarter, rows_at(quarter, piece), first_cols, lambda do: each(quarter, do))

        @pl.when((index >= EARLY) & (index < EARLY + PATCH))
        def _():
            act(
                index - EARLY, N_QUARTER, pl.ds(0, padded), last_cols, lambda do: do(whole_rows)
            )

        @pl.when((index >= EARLY + PATCH) & (index < TICKS))
        def _():
            rel, quarter = piece_of(index - EARLY - PATCH)
            act(rel, quarter, rows_at(quarter, piece), all_cols, lambda do: each(quarter, do))

    def arrive(index):
        @pl.when((index < EARLY) & (lax.rem(index, 2) == 1))
        def _():
            quarter = lax.div(index, 2)
            each(quarter, lambda rows: landed(1, quarter, rows).wait_recv())

        @pl.when(index == EARLY)
        def _():
            for swap in swaps:
                swap.wait_recv()
            taken = meta[slots - 1, 0:1, 0:1] > 0.0
            meta[slots - 1] = jnp.where(taken, meta[slots - 1], extra_meta[...])
            density[most:] = jnp.where(taken, density[most:], extra[...])
            keep[:, most:] = jnp.where(lanes < meta[slots - 1, 0:1], 1.0, 0.0)

        @pl.when((index >= EARLY + PATCH) & (index < TICKS))
        def _():
            rel, quarter = piece_of(index - EARLY - PATCH)
            each(quarter, lambda rows: landed(rel, quarter, rows).wait_recv())

            @pl.when(lax.rem(rel, 2) == 0)
            def _():
                each(quarter, lambda rows: forward_copy(rel, quarter, rows).start())

            @pl.when((rel == 2) & (quarter == 0))
            def _():
                corner_copy(2, 0, pl.ds(0, piece)).start()

            @pl.when((rel == 4) & (quarter > 0))
            def _():
                each(quarter, lambda rows: corner_copy(4, quarter, rows).start())

    def project(rel, quarter, rows, columns, sizes):
        result = lax.dot_general(
            eig[rel, rows], density[columns], (((1,), (1,)), ((), ())),
            preferred_element_type=jnp.float32,
        )
        part[rel, rows, columns] = result
        sent[rel, rows, columns] = result.astype(jnp.bfloat16)

        @pl.when(edge)
        def _():
            sizes(lambda dma_rows: z_copy(0, rel, quarter, dma_rows, columns).start())

    def add_edge(rel, quarter, rows, columns, sizes):
        sizes(lambda dma_rows: z_copy(0, rel, quarter, dma_rows, columns).wait_recv())
        total = part[rel, rows, columns] + from_edge[rel, rows, columns].astype(jnp.float32)
        part[rel, rows, columns] = total
        sent[rel, rows, columns] = total.astype(jnp.bfloat16)
        sizes(lambda dma_rows: z_copy(1, rel, quarter, dma_rows, columns).start())

    def add_mid(rel, quarter, rows, columns, sizes):
        sizes(lambda dma_rows: z_copy(1, rel, quarter, dma_rows, columns).wait_recv())
        total = part[rel, rows, columns] + from_mid[rel, rows, columns].astype(jnp.float32)
        proj[rel, rows, columns] = (total * keep[0:1, columns]).astype(jnp.bfloat16)
        sizes(lambda dma_rows: z_copy(2, rel, quarter, dma_rows, columns).start())

    def apply_screen(rel, quarter):
        acc[...] += lax.dot_general(
            proj[rel, rows_at(quarter, piece)], screen[flip(band, rel), quarter],
            (((0,), (1,)), ((), ())), preferred_element_type=jnp.float32,
        )

    def screen_early(index):
        rel, quarter = lax.rem(index, 2), lax.div(index, 2)

        @pl.when(edge)
        def _():
            each(quarter, lambda rows: z_copy(2, rel, quarter, rows, first_cols).wait_recv())

            @pl.when(quarter == 0)
            def _():
                z_copy(2, rel, N_QUARTER, whole_rows, last_cols).wait_recv()

        apply_screen(rel, quarter)

    def screen_full(index):
        rel, quarter = piece_of(index)

        @pl.when(edge)
        def _():
            each(quarter, lambda rows: z_copy(2, rel, quarter, rows, all_cols).wait_recv())

        apply_screen(rel, quarter)

    width = screen_ref.shape[0] // 2

    def arrange_screen(at):
        for quarter in range(N_QUARTER):
            rows = piece if quarter < N_QUARTER - 1 else short
            left = at * depth + quarter * piece
            for half in range(2):
                picked = stage[half * width : (half + 1) * width, left : left + rows]
                if rows < piece:
                    picked = jnp.concatenate(
                        [picked, jnp.zeros((width, piece - rows), picked.dtype)], axis=1
                    )
                screen[at, quarter, half * padded : half * padded + width] = picked
                screen[at, quarter, half * padded + width : (half + 1) * padded] = jnp.zeros(
                    (padded - width, piece), picked.dtype
                )

    strip = place.shape[1]

    def build_place():
        for slot in range(slots):
            here = slice(slot * block, (slot + 1) * block)
            window = lax.broadcasted_iota(jnp.int32, (strip, block), 1).astype(jnp.float32)
            window = window + meta[slot, 2:3]
            bands = lax.broadcasted_iota(jnp.int32, (strip, block), 0).astype(jnp.float32)
            for index in range(n_rel):
                same = bands + float(index * strip) == window
                place[index, :, here] = jnp.where(same, 1.0, 0.0).astype(jnp.bfloat16)

    def step(t, carry):
        arrive(t)
        items(t, True, project)

        @pl.when(inner)
        def _():
            items(t - LAG_SUM, True, add_edge)
            items(t - LAG_TOTAL, True, add_mid)

        for at in range(n_rel):
            @pl.when(t == 4 + at)
            def _():
                if at == 0:
                    loads[2].wait()
                arrange_screen(at)

        @pl.when(t == EARLY + 4)
        def _():
            build_place()

        early = t - EARLY - PATCH - LAG_SCREEN

        @pl.when((early >= 0) & (early < EARLY))
        def _():
            screen_early(early)

        full = t - EARLY - PATCH - LAG_SCREEN

        @pl.when((full >= 0) & (full < FULL))
        def _():
            screen_full(full)

        return carry

    loads[0].wait()
    loads[1].wait()
    lax.fori_loop(0, TICKS + LAG_SCREEN, step, 0)

    pair = [proj.at[flip(band, 2 * z + half)] for half in range(2)]
    for slot in range(slots):
        here = slice(slot * block, (slot + 1) * block)
        total = 0.0
        for value in split(acc[here]):
            for half in range(2):
                total = total + jnp.dot(
                    value[:, half * padded : (half + 1) * padded], pair[half][:, here],
                    preferred_element_type=jnp.float32,
                )
        spread = 0.0
        for value in split(total * meta[slot, 1:2]):
            spread = spread + lax.dot_general(
                value, place[:, :, here].reshape(n_rel * strip, block), (((1,), (1,)), ((), ())),
                preferred_element_type=jnp.float32,
            )
        high[here], low[here] = split(spread)

    core = lax.rem(band, 2)
    chip = lax.div(band, 2)

    def strips(parity):
        rows = jnp.concatenate([place[2 * index + parity] for index in range(n_rel // 2)], axis=0)
        return sum(
            jnp.dot(rows, value[...], preferred_element_type=jnp.float32) for value in (high, low)
        ).reshape(sig_out.shape)

    sig_out[...] = strips(1 - core)
    core_copy = remote(sig_out, sig_in, sig_send, sig_recv, (flip(band, 1), z))
    core_copy.start()
    sig_own[...] = strips(core)

    def chip_copy(rel):
        target = flip(band, 2 * rel)
        return remote(
            sig_own.at[lax.div(target, 2)], xy_in.at[rel - 1], xy_send.at[rel - 1],
            xy_recv.at[rel - 1], (target, z),
        )

    def final_copy(k):
        target = lax.rem(z + k, n_z)
        return remote(
            band_sum.at[target], fin_in.at[k - 1], fin_send.at[k - 1], fin_recv.at[k - 1],
            (band, target),
        )

    core_copy.wait_recv()
    sig_own[...] += sig_in[...]
    for rel in (3, 1, 2):
        chip_copy(rel).start()

    for swap in swaps:
        swap.wait_send()

    def drain(rel, carry):
        for quarter in range(N_QUARTER):
            rows = rows_at(quarter, piece if quarter < N_QUARTER - 1 else short)

            @pl.when(rel > 0)
            def _():
                landed(rel, quarter, rows).wait_send()

            def drain_z(columns):
                @pl.when(edge)
                def _():
                    z_copy(0, rel, quarter, rows, columns).wait_send()

                @pl.when(inner)
                def _():
                    z_copy(1, rel, quarter, rows, columns).wait_send()
                    z_copy(2, rel, quarter, rows, columns).wait_send()

            @pl.when(rel < 2)
            def _():
                drain_z(first_cols)

            @pl.when(rel >= 2)
            def _():
                drain_z(all_cols)

        @pl.when((rel < 2) & edge)
        def _():
            z_copy(0, rel, N_QUARTER, whole_rows, last_cols).wait_send()

        @pl.when((rel < 2) & inner)
        def _():
            z_copy(1, rel, N_QUARTER, whole_rows, last_cols).wait_send()
            z_copy(2, rel, N_QUARTER, whole_rows, last_cols).wait_send()

        return carry

    lax.fori_loop(0, n_rel, drain, 0)
    core_copy.wait_send()

    total = sig_own[chip]
    for rel in range(1, 4):
        chip_copy(rel).wait_recv()
        total = total + xy_in[rel - 1]
    band_sum[...] = total.reshape(band_sum.shape)
    for k in (2, 1, 3):
        final_copy(k).start()
    total = band_sum[z]
    for k in range(1, n_z):
        final_copy(k).wait_recv()
        total = total + fin_in[k - 1]
    out_ref[...] = total
    for rel in range(1, 4):
        chip_copy(rel).wait_send()
    for k in range(1, n_z):
        final_copy(k).wait_send()


def per_device(
    n_z, n_rel, pair_density, eigvecs, screening, occupation, window_start, window_len, slot_band
):
    capacity, block, plane_rows = pair_density.shape
    depth, width = eigvecs.shape[0], screening.shape[0]
    slots = capacity - 1
    cols = slots * block
    piece = -(-depth // (16 * N_QUARTER)) * 16
    padded = N_QUARTER * piece
    dma = pltpu.SemaphoreType.DMA
    vmem = pl.BlockSpec(memory_space=pltpu.VMEM)
    smem = pl.BlockSpec(memory_space=pltpu.SMEM)
    hbm = pl.BlockSpec(memory_space=pl.ANY)
    strip = NB_SIGMA // n_rel
    fine = strip // n_z
    f32, bf16 = jnp.float32, jnp.bfloat16
    return pl.pallas_call(
        fused_kernel,
        out_shape=jax.ShapeDtypeStruct((fine, NB_SIGMA), f32),
        in_specs=[hbm, hbm, hbm, smem, smem, smem, smem],
        out_specs=vmem,
        scratch_shapes=[
            pltpu.VMEM((cols, plane_rows), bf16),
            pltpu.VMEM((block, plane_rows), bf16),
            pltpu.VMEM((8, block), f32),
            pltpu.VMEM((8, block), f32),
            pltpu.VMEM((slots, 8, block), f32),
            pltpu.VMEM((8, cols), f32),
            pltpu.VMEM((n_rel, padded, plane_rows), bf16),
            pltpu.VMEM((width, screening.shape[1]), bf16),
            pltpu.VMEM((n_rel, N_QUARTER, 2 * padded, piece), bf16),
            pltpu.VMEM((n_rel, padded, cols), f32),
            pltpu.VMEM((n_rel, padded, cols), bf16),
            pltpu.VMEM((n_rel, padded, cols), bf16),
            pltpu.VMEM((n_rel, padded, cols), bf16),
            pltpu.VMEM((n_rel, padded, cols), bf16),
            pltpu.VMEM((cols, 2 * padded), f32),
            pltpu.VMEM((n_rel, strip, cols), bf16),
            pltpu.VMEM((cols, NB_SIGMA), bf16),
            pltpu.VMEM((cols, NB_SIGMA), bf16),
            pltpu.VMEM((n_rel // 2, strip, NB_SIGMA), f32),
            pltpu.VMEM((n_rel // 2, strip, NB_SIGMA), f32),
            pltpu.VMEM((n_rel // 2, strip, NB_SIGMA), f32),
            pltpu.VMEM((n_rel // 2 - 1, strip, NB_SIGMA), f32),
            pltpu.VMEM((n_z, fine, NB_SIGMA), f32),
            pltpu.VMEM((n_z - 1, fine, NB_SIGMA), f32),
            dma((3,)),
            dma((2,)),
            dma((2,)),
            dma((n_rel, N_QUARTER)),
            dma((n_rel, N_QUARTER)),
            dma((3, n_rel, N_QUARTER + 1)),
            dma((3, n_rel, N_QUARTER + 1)),
            dma,
            dma,
            dma((n_rel // 2 - 1,)),
            dma((n_rel // 2 - 1,)),
            dma((n_z - 1,)),
            dma((n_z - 1,)),
        ],
        compiler_params=pltpu.CompilerParams(
            collective_id=0, has_side_effects=True, vmem_limit_bytes=60 * 2**20
        ),
    )(
        pair_density.reshape(capacity * block, plane_rows),
        eigvecs,
        screening,
        window_start,
        window_len,
        slot_band,
        occupation,
    )


def solution(mesh):
    n_band, n_z = mesh.shape["band"], mesh.shape["pw"]
    body = ring_per_device
    if n_band == 8 and n_z == 4:
        body = functools.partial(per_device, n_z, n_band)
    return jax.shard_map(
        body,
        mesh=mesh,
        in_specs=(
            P("band", None, "pw"),
            P("band", "pw"),
            P("pw", None),
            P(),
            P("band"),
            P("band"),
            P("band"),
        ),
        out_specs=P(("band", "pw"), None),
        check_vma=False,
    )
```

time: 159 us -> 112 us (0.70)
  Pallas kernels: 155 us -> 109 us
    pallas_call x1, Pallas kernels: 155 us -> 109 us  [per_device(): pl.pallas_call(fused_kernel, out_shape=jax.ShapeDtypeStruct((fine, NB_SIG...]
where the time goes in v1:
time: 112 us; the launch traced here: 110 us
  Pallas kernels  109 us (97%)
  local copies, waits for them, and re-layouts  1.38 us (1%)
    pallas_call x1, Pallas kernels, per_device(): pl.pallas_call(fused_kernel, out_shape=jax.ShapeDtypeStruct((fine, NB_SIG...  109 us

profile of v1, /device:TPU:1, one launch (start us, length us, event | category | flops | bytes accessed | tf_op | source)
XLA Modules:
  0.0 110.4 jit_solution(4063925318913358239)
XLA Ops:
  0.0 109.0 %shard_map.73 = f32[16,512]{1,0:T(8,128)} custom-call(bf16[640,2304]{1,0:T(8,128)(2,1)} %bitcast.1, bf16[368,2304]{1,0:T(8,128)(2,1)} %eig_ref.1, bf16[736,2944]{1,0:T(8,128)(2,1)} %screen_ref.1, s32[5]{0:T(128)} %start_ref.1, s32[5]{0:T(128)} %len_ref.1, s32[5]{0:T(128)} %slot_ref.1, f32[16]{0:T(128)} %occ_ref.1), custom_call_target="tpu_custom_call" | custom-call | tf_op jit(solution)/shard_map/pallas_call | solution.py:516
  109.0 1.4 %copy.9 = f32[16,512]{1,0:T(8,128)} copy(f32[16,512]{1,0:T(8,128)} %shard_map.73) | data formatting | bytes 65536

commit v2 on v1

--- a/solution.py
+++ b/solution.py
@@ -71,7 +71,14 @@
 N_QUARTER = 4
 EARLY, PATCH, FULL = 2 * N_QUARTER, 2, 6 * N_QUARTER
 TICKS = EARLY + PATCH + FULL
-LAG_SUM, LAG_TOTAL, LAG_SCREEN = 2, 5, 8
+LAG_SUM, LAG_TOTAL, LAG_SCREEN = 2, 4, 6
+DONE = (8, 9, 20, 21, 24, 25, 32, 33)
+
+
+def quarter_sizes(depth):
+    units = depth // 16
+    middle = -(-units // N_QUARTER)
+    return 16 * (middle + 1), 16 * middle, 16 * middle, 16 * (units - 3 * middle - 1)
 
 
 def piece_of(order):
@@ -87,17 +94,18 @@
 
 def fused_kernel(
     density_ref, eig_ref, screen_ref, start_ref, len_ref, slot_ref, occ_ref, out_ref,
-    density, extra, extra_out, extra_meta, meta, keep, eig, stage, screen, part, sent, from_edge, from_mid,
-    proj, acc, place, high, low, sig_out, sig_own, sig_in, xy_in, band_sum, fin_in,
+    density, extra, extra_out, extra_meta, meta, keep, eig, screen, part, sent, from_edge, from_mid,
+    proj, acc, place, high, low, sig_out, sig_own, sig_in, xy_out, xy_in, band_sum, fin_in,
     load_sem, swap_send, swap_recv, eig_send, eig_recv, z_send, z_recv, sig_send, sig_recv, xy_send, xy_recv,
     fin_send, fin_recv,
 ):
     mesh_id = pl.DeviceIdType.MESH
     band, z = lax.axis_index("band"), lax.axis_index("pw")
-    n_rel, padded, _ = eig.shape
-    depth = eig_ref.shape[0]
-    piece = padded // N_QUARTER
-    short = depth - (N_QUARTER - 1) * piece
+    n_rel, depth, _ = eig.shape
+    sizes = quarter_sizes(depth)
+    span = proj.shape[1]
+    padded = acc.shape[1] // 2
+    half_rows = screen_ref.shape[0] // 2
     block = extra.shape[0]
     cols = density.shape[0]
     slots = cols // block
@@ -109,11 +117,17 @@
     whole_rows = pl.ds(0, depth)
 
     loads = [
-        pltpu.make_async_copy(eig_ref, eig.at[0, whole_rows], load_sem.at[0]),
+        pltpu.make_async_copy(eig_ref, eig.at[0], load_sem.at[0]),
         pltpu.make_async_copy(density_ref.at[pl.ds(0, cols)], density, load_sem.at[1]),
-        pltpu.make_async_copy(screen_ref, stage, load_sem.at[2]),
+    ] + [
+        pltpu.make_async_copy(
+            screen_ref.at[pl.ds(half * half_rows, half_rows)],
+            screen.at[pl.ds(half * padded, half_rows), pl.ds(0, screen_ref.shape[1])],
+            load_sem.at[2 + half],
+        )
+        for half in range(2)
     ]
-    for load in loads:
+    for load in loads[:2]:
         load.start()
 
     def fields(slot):
@@ -135,12 +149,6 @@
         pl.semaphore_signal(
             barrier, inc=1, device_id=(band, lax.rem(z + k, n_z)), device_id_type=mesh_id
         )
-    tail = pl.ds(depth, padded - depth)
-    for rel in range(n_rel):
-        eig[rel, tail] = jnp.zeros((padded - depth, eig.shape[2]), eig.dtype)
-        for buffer in (from_edge, from_mid, proj):
-            buffer[rel, tail] = jnp.zeros((padded - depth, cols), buffer.dtype)
-    acc[...] = jnp.zeros_like(acc)
     lanes = lax.broadcasted_iota(jnp.int32, (8, block), 1).astype(jnp.float32)
     for slot in range(slots):
         keep[:, slot * block : (slot + 1) * block] = jnp.where(lanes < meta[slot, 0:1], 1.0, 0.0)
@@ -152,23 +160,27 @@
             device_id=device, device_id_type=mesh_id,
         )
 
-    def rows_at(quarter, rows):
+    def first_row(quarter):
         if isinstance(quarter, int):
-            return pl.ds(quarter * piece, rows)
-        return pl.ds(pl.multiple_of(quarter * piece, 16), rows)
+            return sum(sizes[:quarter])
+        return pl.multiple_of(
+            quarter * sizes[1] + lax.div(quarter + 3, 4) * (sizes[0] - sizes[1]), 16
+        )
 
     def each(quarter, act):
         if isinstance(quarter, int):
-            act(rows_at(quarter, piece if quarter < N_QUARTER - 1 else short))
+            act(pl.ds(first_row(quarter), sizes[quarter]))
             return
-
-        @pl.when(quarter < N_QUARTER - 1)
-        def _():
-            act(rows_at(quarter, piece))
-
-        @pl.when(quarter == N_QUARTER - 1)
-        def _():
-            act(rows_at(quarter, short))
+        for first, stop in ((0, 1), (1, 3), (3, 4)):
+            @pl.when((quarter >= first) & (quarter < stop))
+            def _():
+                act(pl.ds(first_row(quarter), sizes[first]))
+
+    def lane_of(rel):
+        return flip(band, rel) * depth
+
+    def shifted(rel, rows):
+        return pl.ds(pl.multiple_of(rows.start + lax.rem(lane_of(rel), 128), 16), rows.size)
 
     def own_copy(rel, quarter, rows):
         return remote(
@@ -196,6 +208,8 @@
 
     def z_copy(kind, rel, quarter, rows, columns):
         source, target = ((sent, from_edge), (sent, from_mid), (proj, proj))[kind]
+        if kind == 2:
+            rows = shifted(rel, rows)
         return remote(
             source.at[rel, rows, columns], target.at[rel, rows, columns],
             z_send.at[kind, rel, quarter], z_recv.at[kind, rel, quarter],
@@ -216,22 +230,30 @@
 
     first_cols, last_cols, all_cols = pl.ds(0, most), pl.ds(most, block), pl.ds(0, cols)
 
-    def items(index, whole, act):
+    proj[...] = jnp.zeros_like(proj)
+    acc[...] = jnp.zeros_like(acc)
+    for half in range(2):
+        screen[half * padded + half_rows : (half + 1) * padded] = jnp.zeros(
+            (padded - half_rows, screen.shape[1]), screen.dtype
+        )
+    screen[:, screen_ref.shape[1] :] = jnp.zeros(
+        (screen.shape[0], screen.shape[1] - screen_ref.shape[1]), screen.dtype
+    )
+
+    def items(index, act):
         @pl.when((index >= 0) & (index < EARLY))
         def _():
             rel, quarter = lax.rem(index, 2), lax.div(index, 2)
-            act(rel, quarter, rows_at(quarter, piece), first_cols, lambda do: each(quarter, do))
+            each(quarter, lambda rows: act(rel, quarter, rows, first_cols))
 
         @pl.when((index >= EARLY) & (index < EARLY + PATCH))
         def _():
-            act(
-                index - EARLY, N_QUARTER, pl.ds(0, padded), last_cols, lambda do: do(whole_rows)
-            )
+            act(index - EARLY, N_QUARTER, whole_rows, last_cols)
 
         @pl.when((index >= EARLY + PATCH) & (index < TICKS))
         def _():
             rel, quarter = piece_of(index - EARLY - PATCH)
-            act(rel, quarter, rows_at(quarter, piece), all_cols, lambda do: each(quarter, do))
+            each(quarter, lambda rows: act(rel, quarter, rows, all_cols))
 
     def arrive(index):
         @pl.when((index < EARLY) & (lax.rem(index, 2) == 1))
@@ -259,13 +281,13 @@
 
             @pl.when((rel == 2) & (quarter == 0))
             def _():
-                corner_copy(2, 0, pl.ds(0, piece)).start()
+                each(0, lambda rows: corner_copy(2, 0, rows).start())
 
             @pl.when((rel == 4) & (quarter > 0))
             def _():
                 each(quarter, lambda rows: corner_copy(4, quarter, rows).start())
 
-    def project(rel, quarter, rows, columns, sizes):
+    def project(rel, quarter, rows, columns):
         result = lax.dot_general(
             eig[rel, rows], density[columns], (((1,), (1,)), ((), ())),
             preferred_element_type=jnp.float32,
@@ -275,65 +297,42 @@
 
         @pl.when(edge)
         def _():
-            sizes(lambda dma_rows: z_copy(0, rel, quarter, dma_rows, columns).start())
-
-    def add_edge(rel, quarter, rows, columns, sizes):
-        sizes(lambda dma_rows: z_copy(0, rel, quarter, dma_rows, columns).wait_recv())
+            z_copy(0, rel, quarter, rows, columns).start()
+
+    def add_edge(rel, quarter, rows, columns):
+        z_copy(0, rel, quarter, rows, columns).wait_recv()
         total = part[rel, rows, columns] + from_edge[rel, rows, columns].astype(jnp.float32)
         part[rel, rows, columns] = total
         sent[rel, rows, columns] = total.astype(jnp.bfloat16)
-        sizes(lambda dma_rows: z_copy(1, rel, quarter, dma_rows, columns).start())
-
-    def add_mid(rel, quarter, rows, columns, sizes):
-        sizes(lambda dma_rows: z_copy(1, rel, quarter, dma_rows, columns).wait_recv())
+        z_copy(1, rel, quarter, rows, columns).start()
+
+    def add_mid(rel, quarter, rows, columns):
+        z_copy(1, rel, quarter, rows, columns).wait_recv()
         total = part[rel, rows, columns] + from_mid[rel, rows, columns].astype(jnp.float32)
-        proj[rel, rows, columns] = (total * keep[0:1, columns]).astype(jnp.bfloat16)
-        sizes(lambda dma_rows: z_copy(2, rel, quarter, dma_rows, columns).start())
-
-    def apply_screen(rel, quarter):
+        proj[rel, shifted(rel, rows), columns] = (total * keep[0:1, columns]).astype(jnp.bfloat16)
+        z_copy(2, rel, quarter, rows, columns).start()
+
+    def apply_screen(rel):
+        @pl.when(edge)
+        def _():
+            for columns, some in ((first_cols, rel < 2), (all_cols, rel >= 2)):
+                @pl.when(some)
+                def _():
+                    for quarter in range(N_QUARTER):
+                        each(
+                            quarter,
+                            lambda rows: z_copy(2, rel, quarter, rows, columns).wait_recv(),
+                        )
+
+            @pl.when(rel < 2)
+            def _():
+                z_copy(2, rel, N_QUARTER, whole_rows, last_cols).wait_recv()
+
+        lane = pl.multiple_of(lax.div(lane_of(rel), 128) * 128, 128)
         acc[...] += lax.dot_general(
-            proj[rel, rows_at(quarter, piece)], screen[flip(band, rel), quarter],
+            proj[rel], screen[:, pl.ds(lane, span)],
             (((0,), (1,)), ((), ())), preferred_element_type=jnp.float32,
         )
-
-    def screen_early(index):
-        rel, quarter = lax.rem(index, 2), lax.div(index, 2)
-
-        @pl.when(edge)
-        def _():
-            each(quarter, lambda rows: z_copy(2, rel, quarter, rows, first_cols).wait_recv())
-
-            @pl.when(quarter == 0)
-            def _():
-                z_copy(2, rel, N_QUARTER, whole_rows, last_cols).wait_recv()
-
-        apply_screen(rel, quarter)
-
-    def screen_full(index):
-        rel, quarter = piece_of(index)
-
-        @pl.when(edge)
-        def _():
-            each(quarter, lambda rows: z_copy(2, rel, quarter, rows, all_cols).wait_recv())
-
-        apply_screen(rel, quarter)
-
-    width = screen_ref.shape[0] // 2
-
-    def arrange_screen(at):
-        for quarter in range(N_QUARTER):
-            rows = piece if quarter < N_QUARTER - 1 else short
-            left = at * depth + quarter * piece
-            for half in range(2):
-                picked = stage[half * width : (half + 1) * width, left : left + rows]
-                if rows < piece:
-                    picked = jnp.concatenate(
-                        [picked, jnp.zeros((width, piece - rows), picked.dtype)], axis=1
-                    )
-                screen[at, quarter, half * padded : half * padded + width] = picked
-                screen[at, quarter, half * padded + width : (half + 1) * padded] = jnp.zeros(
-                    (padded - width, piece), picked.dtype
-                )
 
     strip = place.shape[1]
 
@@ -349,59 +348,57 @@
 
     def step(t, carry):
         arrive(t)
-        items(t, True, project)
+        items(t, project)
 
         @pl.when(inner)
         def _():
-            items(t - LAG_SUM, True, add_edge)
-            items(t - LAG_TOTAL, True, add_mid)
-
-        for at in range(n_rel):
-            @pl.when(t == 4 + at)
-            def _():
-                if at == 0:
-                    loads[2].wait()
-                arrange_screen(at)
+            items(t - LAG_SUM, add_edge)
+            items(t - LAG_TOTAL, add_mid)
 
         @pl.when(t == EARLY + 4)
         def _():
             build_place()
-
-        early = t - EARLY - PATCH - LAG_SCREEN
-
-        @pl.when((early >= 0) & (early < EARLY))
-        def _():
-            screen_early(early)
-
-        full = t - EARLY - PATCH - LAG_SCREEN
-
-        @pl.when((full >= 0) & (full < FULL))
-        def _():
-            screen_full(full)
+            for load in loads[2:]:
+                load.wait()
+
+        done = t - LAG_SCREEN
+        ready = done == DONE[0]
+        for index in DONE[1:]:
+            ready = ready | (done == index)
+
+        @pl.when(ready)
+        def _():
+            late = lax.div(done, EARLY + PATCH)
+            late = lax.div(late + 3, 4)
+            apply_screen(
+                (1 - late) * (done - EARLY) + late * piece_of(late * (done - EARLY - PATCH))[0]
+            )
 
         return carry
 
     loads[0].wait()
     loads[1].wait()
+    for load in loads[2:]:
+        load.start()
     lax.fori_loop(0, TICKS + LAG_SCREEN, step, 0)
 
-    pair = [proj.at[flip(band, 2 * z + half)] for half in range(2)]
+    pair = []
+    for half in range(2):
+        rel = flip(band, 2 * z + half)
+        pair.append((rel, shifted(rel, pl.ds(0, padded))))
     for slot in range(slots):
         here = slice(slot * block, (slot + 1) * block)
-        total = 0.0
-        for value in split(acc[here]):
-            for half in range(2):
-                total = total + jnp.dot(
-                    value[:, half * padded : (half + 1) * padded], pair[half][:, here],
-                    preferred_element_type=jnp.float32,
-                )
-        spread = 0.0
-        for value in split(total * meta[slot, 1:2]):
-            spread = spread + lax.dot_general(
-                value, place[:, :, here].reshape(n_rel * strip, block), (((1,), (1,)), ((), ())),
-                preferred_element_type=jnp.float32,
-            )
-        high[here], low[here] = split(spread)
+        other = jnp.concatenate([proj[rel, rows, here] for rel, rows in pair], axis=0)
+        total = jnp.dot(
+            jnp.concatenate(split(acc[here]), axis=0), other, preferred_element_type=jnp.float32
+        )
+        total = (total[:block] + total[block:]) * meta[slot, 1:2]
+        spread = lax.dot_general(
+            jnp.concatenate(split(total), axis=0),
+            place[:, :, here].reshape(n_rel * strip, block), (((1,), (1,)), ((), ())),
+            preferred_element_type=jnp.float32,
+        )
+        high[here], low[here] = split(spread[:block] + spread[block:])
 
     core = lax.rem(band, 2)
     chip = lax.div(band, 2)
@@ -420,7 +417,7 @@
     def chip_copy(rel):
         target = flip(band, 2 * rel)
         return remote(
-            sig_own.at[lax.div(target, 2)], xy_in.at[rel - 1], xy_send.at[rel - 1],
+            xy_out.at[lax.div(target, 2)], xy_in.at[rel - 1], xy_send.at[rel - 1],
             xy_recv.at[rel - 1], (target, z),
         )
 
@@ -433,46 +430,40 @@
 
     core_copy.wait_recv()
     sig_own[...] += sig_in[...]
+    xy_out[...] = sig_own[...].astype(jnp.bfloat16)
     for rel in (3, 1, 2):
         chip_copy(rel).start()
 
     for swap in swaps:
         swap.wait_send()
 
+    def drain_z(rel, quarter, rows, columns):
+        @pl.when(edge)
+        def _():
+            z_copy(0, rel, quarter, rows, columns).wait_send()
+
+        @pl.when(inner)
+        def _():
+            z_copy(1, rel, quarter, rows, columns).wait_send()
+            z_copy(2, rel, quarter, rows, columns).wait_send()
+
     def drain(rel, carry):
         for quarter in range(N_QUARTER):
-            rows = rows_at(quarter, piece if quarter < N_QUARTER - 1 else short)
-
             @pl.when(rel > 0)
             def _():
-                landed(rel, quarter, rows).wait_send()
-
-            def drain_z(columns):
-                @pl.when(edge)
-                def _():
-                    z_copy(0, rel, quarter, rows, columns).wait_send()
-
-                @pl.when(inner)
-                def _():
-                    z_copy(1, rel, quarter, rows, columns).wait_send()
-                    z_copy(2, rel, quarter, rows, columns).wait_send()
+                each(quarter, lambda rows: landed(rel, quarter, rows).wait_send())
 
             @pl.when(rel < 2)
             def _():
-                drain_z(first_cols)
+                each(quarter, lambda rows: drain_z(rel, quarter, rows, first_cols))
 
             @pl.when(rel >= 2)
             def _():
-                drain_z(all_cols)
-
-        @pl.when((rel < 2) & edge)
-        def _():
-            z_copy(0, rel, N_QUARTER, whole_rows, last_cols).wait_send()
-
-        @pl.when((rel < 2) & inner)
-        def _():
-            z_copy(1, rel, N_QUARTER, whole_rows, last_cols).wait_send()
-            z_copy(2, rel, N_QUARTER, whole_rows, last_cols).wait_send()
+                each(quarter, lambda rows: drain_z(rel, quarter, rows, all_cols))
+
+        @pl.when(rel < 2)
+        def _():
+            drain_z(rel, N_QUARTER, whole_rows, last_cols)
 
         return carry
 
@@ -482,7 +473,7 @@
     total = sig_own[chip]
     for rel in range(1, 4):
         chip_copy(rel).wait_recv()
-        total = total + xy_in[rel - 1]
+        total = total + xy_in[rel - 1].astype(jnp.float32)
     band_sum[...] = total.reshape(band_sum.shape)
     for k in (2, 1, 3):
         final_copy(k).start()
@@ -504,8 +495,9 @@
     depth, width = eigvecs.shape[0], screening.shape[0]
     slots = capacity - 1
     cols = slots * block
-    piece = -(-depth // (16 * N_QUARTER)) * 16
-    padded = N_QUARTER * piece
+    half_rows = -(-(width // 2) // 128) * 128
+    span = -(-(depth + 112) // 128) * 128
+    lanes = -(-screening.shape[1] // 128) * 128 + 128
     dma = pltpu.SemaphoreType.DMA
     vmem = pl.BlockSpec(memory_space=pltpu.VMEM)
     smem = pl.BlockSpec(memory_space=pltpu.SMEM)
@@ -525,25 +517,25 @@
             pltpu.VMEM((8, block), f32),
             pltpu.VMEM((slots, 8, block), f32),
             pltpu.VMEM((8, cols), f32),
-            pltpu.VMEM((n_rel, padded, plane_rows), bf16),
-            pltpu.VMEM((width, screening.shape[1]), bf16),
-            pltpu.VMEM((n_rel, N_QUARTER, 2 * padded, piece), bf16),
-            pltpu.VMEM((n_rel, padded, cols), f32),
-            pltpu.VMEM((n_rel, padded, cols), bf16),
-            pltpu.VMEM((n_rel, padded, cols), bf16),
-            pltpu.VMEM((n_rel, padded, cols), bf16),
-            pltpu.VMEM((n_rel, padded, cols), bf16),
-            pltpu.VMEM((cols, 2 * padded), f32),
+            pltpu.VMEM((n_rel, depth, plane_rows), bf16),
+            pltpu.VMEM((2 * half_rows, lanes), bf16),
+            pltpu.VMEM((n_rel, depth, cols), f32),
+            pltpu.VMEM((n_rel, depth, cols), bf16),
+            pltpu.VMEM((n_rel, depth, cols), bf16),
+            pltpu.VMEM((n_rel, depth, cols), bf16),
+            pltpu.VMEM((n_rel, span, cols), bf16),
+            pltpu.VMEM((cols, 2 * half_rows), f32),
             pltpu.VMEM((n_rel, strip, cols), bf16),
             pltpu.VMEM((cols, NB_SIGMA), bf16),
             pltpu.VMEM((cols, NB_SIGMA), bf16),
             pltpu.VMEM((n_rel // 2, strip, NB_SIGMA), f32),
             pltpu.VMEM((n_rel // 2, strip, NB_SIGMA), f32),
             pltpu.VMEM((n_rel // 2, strip, NB_SIGMA), f32),
-            pltpu.VMEM((n_rel // 2 - 1, strip, NB_SIGMA), f32),
+            pltpu.VMEM((n_rel // 2, strip, NB_SIGMA), bf16),
+            pltpu.VMEM((n_rel // 2 - 1, strip, NB_SIGMA), bf16),
             pltpu.VMEM((n_z, fine, NB_SIGMA), f32),
             pltpu.VMEM((n_z - 1, fine, NB_SIGMA), f32),
-            dma((3,)),
+            dma((4,)),
             dma((2,)),
             dma((2,)),
             dma((n_rel, N_QUARTER)),

time: 112 us -> 109 us (0.973)
  Pallas kernels: 109 us -> 106 us
    pallas_call x1, Pallas kernels: 109 us -> 106 us  [per_device(): pl.pallas_call(fused_kernel, out_shape=jax.ShapeDtypeStruct((fine, NB_SIG...]
where the time goes in v2:
time: 109 us; the launch traced here: 107 us
  Pallas kernels  106 us (97%)
  local copies, waits for them, and re-layouts  1.38 us (1%)
    pallas_call x1, Pallas kernels, per_device(): pl.pallas_call(fused_kernel, out_shape=jax.ShapeDtypeStruct((fine, NB_SIG...  106 us

profile of v2, /device:TPU:1, one launch (start us, length us, event | category | flops | bytes accessed | tf_op | source)
XLA Modules:
  0.0 106.9 jit_solution(5008670940774220666)
XLA Ops:
  0.0 105.6 %shard_map.73 = f32[16,512]{1,0:T(8,128)} custom-call(bf16[640,2304]{1,0:T(8,128)(2,1)} %bitcast.1, bf16[368,2304]{1,0:T(8,128)(2,1)} %eig_ref.1, bf16[736,2944]{1,0:T(8,128)(2,1)} %screen_ref.1, s32[5]{0:T(128)} %start_ref.1, s32[5]{0:T(128)} %len_ref.1, s32[5]{0:T(128)} %slot_ref.1, f32[16]{0:T(128)} %occ_ref.1), custom_call_target="tpu_custom_call" | custom-call | tf_op jit(solution)/shard_map/pallas_call | solution.py:508
  105.6 1.4 %copy.9 = f32[16,512]{1,0:T(8,128)} copy(f32[16,512]{1,0:T(8,128)} %shard_map.73) | data formatting | bytes 65536

commit v3 on v2

--- a/solution.py
+++ b/solution.py
@@ -72,7 +72,22 @@
 EARLY, PATCH, FULL = 2 * N_QUARTER, 2, 6 * N_QUARTER
 TICKS = EARLY + PATCH + FULL
 LAG_SUM, LAG_TOTAL, LAG_SCREEN = 2, 4, 6
-DONE = (8, 9, 20, 21, 24, 25, 32, 33)
+ORDER = (
+    (2, 0), (2, 1), (4, 1), (2, 2), (4, 2), (2, 3), (4, 3), (6, 1), (4, 0), (6, 2), (6, 0), (6, 3),
+)
+DONE = tuple(EARLY + rel for rel in range(2)) + tuple(
+    EARLY + PATCH + 2 * max(at for at, pair in enumerate(ORDER) if pair[0] == rel) + core
+    for rel in (2, 4, 6) for core in range(2)
+)
+
+
+def look_up(values, index):
+    result = values[0]
+    for at in range(1, len(values)):
+        change = values[at] - values[at - 1]
+        if change:
+            result = result + change * lax.div(index + (64 - at), 64)
+    return result
 
 
 def quarter_sizes(depth):
@@ -83,20 +98,15 @@
 
 def piece_of(order):
     pair, core = lax.div(order, 2), lax.rem(order, 2)
-    late = lax.div(pair, 8)
-    side = lax.rem(pair + 1, 2) + lax.div(pair, 7) - 1 + lax.div(pair + 7, 8)
-    near = lax.rem(lax.div(pair + 1, 2), 4)
-    rest = pair - 8 * late
-    corner = lax.rem(rest + 1, 3) + 2 * lax.div(rest, 3)
-    relation = (1 - late) * (2 + 2 * side) + late * 6 + core
-    return relation, (1 - late) * near + late * corner
+    code = look_up([8 * rel + quarter for rel, quarter in ORDER], pair)
+    return lax.div(code, 8) + core, lax.rem(code, 8)
 
 
 def fused_kernel(
     density_ref, eig_ref, screen_ref, start_ref, len_ref, slot_ref, occ_ref, out_ref,
     density, extra, extra_out, extra_meta, meta, keep, eig, screen, part, sent, from_edge, from_mid,
-    proj, acc, place, high, low, sig_out, sig_own, sig_in, xy_out, xy_in, band_sum, fin_in,
-    load_sem, swap_send, swap_recv, eig_send, eig_recv, z_send, z_recv, sig_send, sig_recv, xy_send, xy_recv,
+    proj, acc, place, high, low, sig_out, sig_own, sig_in, fin_out, fin_in,
+    load_sem, swap_send, swap_recv, eig_send, eig_recv, z_send, z_recv, sig_send, sig_recv,
     fin_send, fin_recv,
 ):
     mesh_id = pl.DeviceIdType.MESH
@@ -110,7 +120,8 @@
     cols = density.shape[0]
     slots = cols // block
     most = cols - block
-    n_z = fin_in.shape[0] + 1
+    n_z = fin_out.shape[1]
+    fine = fin_out.shape[2]
     mate, across = z + 1 - 2 * lax.rem(z, 2), n_z - 1 - z
     inner = (z == 1) | (z == 2)
     edge = (z == 0) | (z == n_z - 1)
@@ -152,6 +163,15 @@
     lanes = lax.broadcasted_iota(jnp.int32, (8, block), 1).astype(jnp.float32)
     for slot in range(slots):
         keep[:, slot * block : (slot + 1) * block] = jnp.where(lanes < meta[slot, 0:1], 1.0, 0.0)
+    proj[...] = jnp.zeros_like(proj)
+    acc[...] = jnp.zeros_like(acc)
+    for half in range(2):
+        screen[half * padded + half_rows : (half + 1) * padded] = jnp.zeros(
+            (padded - half_rows, screen.shape[1]), screen.dtype
+        )
+    screen[:, screen_ref.shape[1] :] = jnp.zeros(
+        (screen.shape[0], screen.shape[1] - screen_ref.shape[1]), screen.dtype
+    )
     pl.semaphore_wait(barrier, n_rel - 1 + n_z - 1)
 
     def remote(source, target, send, recv, device):
@@ -229,16 +249,6 @@
             each(quarter, lambda rows: own_copy(rel, quarter, rows).start())
 
     first_cols, last_cols, all_cols = pl.ds(0, most), pl.ds(most, block), pl.ds(0, cols)
-
-    proj[...] = jnp.zeros_like(proj)
-    acc[...] = jnp.zeros_like(acc)
-    for half in range(2):
-        screen[half * padded + half_rows : (half + 1) * padded] = jnp.zeros(
-            (padded - half_rows, screen.shape[1]), screen.dtype
-        )
-    screen[:, screen_ref.shape[1] :] = jnp.zeros(
-        (screen.shape[0], screen.shape[1] - screen_ref.shape[1]), screen.dtype
-    )
 
     def items(index, act):
         @pl.when((index >= 0) & (index < EARLY))
@@ -414,25 +424,22 @@
     core_copy.start()
     sig_own[...] = strips(core)
 
-    def chip_copy(rel):
-        target = flip(band, 2 * rel)
+    def final_copy(rel, k):
+        chip_to, z_to = flip(band, 2 * rel), lax.rem(z + k, n_z)
+        at = rel * n_z + k - 1
         return remote(
-            xy_out.at[lax.div(target, 2)], xy_in.at[rel - 1], xy_send.at[rel - 1],
-            xy_recv.at[rel - 1], (target, z),
-        )
-
-    def final_copy(k):
-        target = lax.rem(z + k, n_z)
-        return remote(
-            band_sum.at[target], fin_in.at[k - 1], fin_send.at[k - 1], fin_recv.at[k - 1],
-            (band, target),
-        )
-
+            fin_out.at[lax.div(chip_to, 2), z_to], fin_in.at[at], fin_send.at[at], fin_recv.at[at],
+            (chip_to, z_to),
+        )
+
+    finals = [
+        final_copy(rel, k) for rel in (3, 1, 2, 0) for k in (2, 1, 3, 0) if rel + k > 0
+    ]
     core_copy.wait_recv()
     sig_own[...] += sig_in[...]
-    xy_out[...] = sig_own[...].astype(jnp.bfloat16)
-    for rel in (3, 1, 2):
-        chip_copy(rel).start()
+    fin_out[...] = sig_own[...].astype(jnp.bfloat16).reshape(fin_out.shape)
+    for copy in finals:
+        copy.start()
 
     for swap in swaps:
         swap.wait_send()
@@ -470,22 +477,14 @@
     lax.fori_loop(0, n_rel, drain, 0)
     core_copy.wait_send()
 
-    total = sig_own[chip]
-    for rel in range(1, 4):
-        chip_copy(rel).wait_recv()
-        total = total + xy_in[rel - 1].astype(jnp.float32)
-    band_sum[...] = total.reshape(band_sum.shape)
-    for k in (2, 1, 3):
-        final_copy(k).start()
-    total = band_sum[z]
-    for k in range(1, n_z):
-        final_copy(k).wait_recv()
-        total = total + fin_in[k - 1]
+    total = sig_own[chip, pl.ds(pl.multiple_of(z * fine, fine), fine)]
+    for copy in finals:
+        copy.wait_recv()
+    for at in range(fin_in.shape[0]):
+        total = total + fin_in[at].astype(jnp.float32)
     out_ref[...] = total
-    for rel in range(1, 4):
-        chip_copy(rel).wait_send()
-    for k in range(1, n_z):
-        final_copy(k).wait_send()
+    for copy in finals:
+        copy.wait_send()
 
 
 def per_device(
@@ -531,10 +530,8 @@
             pltpu.VMEM((n_rel // 2, strip, NB_SIGMA), f32),
             pltpu.VMEM((n_rel // 2, strip, NB_SIGMA), f32),
             pltpu.VMEM((n_rel // 2, strip, NB_SIGMA), f32),
-            pltpu.VMEM((n_rel // 2, strip, NB_SIGMA), bf16),
-            pltpu.VMEM((n_rel // 2 - 1, strip, NB_SIGMA), bf16),
-            pltpu.VMEM((n_z, fine, NB_SIGMA), f32),
-            pltpu.VMEM((n_z - 1, fine, NB_SIGMA), f32),
+            pltpu.VMEM((n_rel // 2, n_z, fine, NB_SIGMA), bf16),
+            pltpu.VMEM((n_rel // 2 * n_z - 1, fine, NB_SIGMA), bf16),
             dma((4,)),
             dma((2,)),
             dma((2,)),
@@ -544,10 +541,8 @@
             dma((3, n_rel, N_QUARTER + 1)),
             dma,
             dma,
-            dma((n_rel // 2 - 1,)),
-            dma((n_rel // 2 - 1,)),
-            dma((n_z - 1,)),
-            dma((n_z - 1,)),
+            dma((n_rel // 2 * n_z - 1,)),
+            dma((n_rel // 2 * n_z - 1,)),
         ],
         compiler_params=pltpu.CompilerParams(
             collective_id=0, has_side_effects=True, vmem_limit_bytes=60 * 2**20

time: 109 us -> 103 us (0.945); the launches traced: 107 us -> 103 us
  Pallas kernels: 106 us -> 101 us
    pallas_call x1, Pallas kernels: 106 us -> 101 us  [per_device(): pl.pallas_call(fused_kernel, out_shape=jax.ShapeDtypeStruct((fine, NB_SIG...]
where the time goes in v3:
time: 103 us
  Pallas kernels  101 us (98%)
  local copies, waits for them, and re-layouts  1.38 us (1%)
    pallas_call x1, Pallas kernels, per_device(): pl.pallas_call(fused_kernel, out_shape=jax.ShapeDtypeStruct((fine, NB_SIG...  101 us

profile of v3, /device:TPU:1, one launch (start us, length us, event | category | flops | bytes accessed | tf_op | source)
XLA Modules:
  0.0 102.7 jit_solution(5497785642726297994)
XLA Ops:
  0.0 101.3 %shard_map.73 = f32[16,512]{1,0:T(8,128)} custom-call(bf16[640,2304]{1,0:T(8,128)(2,1)} %bitcast.1, bf16[368,2304]{1,0:T(8,128)(2,1)} %eig_ref.1, bf16[736,2944]{1,0:T(8,128)(2,1)} %screen_ref.1, s32[5]{0:T(128)} %start_ref.1, s32[5]{0:T(128)} %len_ref.1, s32[5]{0:T(128)} %slot_ref.1, f32[16]{0:T(128)} %occ_ref.1), custom_call_target="tpu_custom_call" | custom-call | tf_op jit(solution)/shard_map/pallas_call | solution.py:507
  101.3 1.4 %copy.9 = f32[16,512]{1,0:T(8,128)} copy(f32[16,512]{1,0:T(8,128)} %shard_map.73) | data formatting | bytes 65536

commit v4 on v3

--- a/solution.py
+++ b/solution.py
@@ -103,7 +103,8 @@
 
 
 def fused_kernel(
-    density_ref, eig_ref, screen_ref, start_ref, len_ref, slot_ref, occ_ref, out_ref,
+    density_ref, eig_ref, screen_ref, start_hbm, len_hbm, slot_hbm, occ_hbm, out_ref,
+    start_ref, len_ref, slot_ref, occ_ref,
     density, extra, extra_out, extra_meta, meta, keep, eig, screen, part, sent, from_edge, from_mid,
     proj, acc, place, high, low, sig_out, sig_own, sig_in, fin_out, fin_in,
     load_sem, swap_send, swap_recv, eig_send, eig_recv, z_send, z_recv, sig_send, sig_recv,
@@ -138,7 +139,13 @@
         )
         for half in range(2)
     ]
-    for load in loads[:2]:
+    tables = [
+        pltpu.make_async_copy(source, target, load_sem.at[4 + index])
+        for index, (source, target) in enumerate(
+            [(start_hbm, start_ref), (len_hbm, len_ref), (slot_hbm, slot_ref), (occ_hbm, occ_ref)]
+        )
+    ]
+    for load in tables + loads[:2]:
         load.start()
 
     def fields(slot):
@@ -149,20 +156,14 @@
         row = lax.broadcasted_iota(jnp.int32, (8, block), 0)
         return jnp.where(row == 0, kept, jnp.where(row == 1, weight, first))
 
-    extra_out[...] = fields(slots)
-    for slot in range(slots):
-        meta[slot] = fields(slot)
-
     barrier = pltpu.get_barrier_semaphore()
-    for rel in range(1, n_rel):
-        pl.semaphore_signal(barrier, inc=1, device_id=(flip(band, rel), z), device_id_type=mesh_id)
-    for k in range(1, n_z):
-        pl.semaphore_signal(
-            barrier, inc=1, device_id=(band, lax.rem(z + k, n_z)), device_id_type=mesh_id
-        )
-    lanes = lax.broadcasted_iota(jnp.int32, (8, block), 1).astype(jnp.float32)
-    for slot in range(slots):
-        keep[:, slot * block : (slot + 1) * block] = jnp.where(lanes < meta[slot, 0:1], 1.0, 0.0)
+    for device in ((flip(band, 1), z), (flip(band, 2), z), (flip(band, 4), z), (band, mate)):
+        pl.semaphore_signal(barrier, inc=1, device_id=device, device_id_type=mesh_id)
+
+    @pl.when(inner)
+    def _():
+        pl.semaphore_signal(barrier, inc=1, device_id=(band, across), device_id_type=mesh_id)
+
     proj[...] = jnp.zeros_like(proj)
     acc[...] = jnp.zeros_like(acc)
     for half in range(2):
@@ -172,7 +173,23 @@
     screen[:, screen_ref.shape[1] :] = jnp.zeros(
         (screen.shape[0], screen.shape[1] - screen_ref.shape[1]), screen.dtype
     )
-    pl.semaphore_wait(barrier, n_rel - 1 + n_z - 1)
+
+    for load in tables:
+        load.wait()
+    extra_out[...] = fields(slots)
+    for slot in range(slots):
+        meta[slot] = fields(slot)
+    lanes = lax.broadcasted_iota(jnp.int32, (8, block), 1).astype(jnp.float32)
+    for slot in range(slots):
+        keep[:, slot * block : (slot + 1) * block] = jnp.where(lanes < meta[slot, 0:1], 1.0, 0.0)
+    @pl.when(edge)
+    def _():
+        pl.semaphore_wait(barrier, 4)
+
+    @pl.when(inner)
+    def _():
+        pl.semaphore_wait(barrier, 5)
+
 
     def remote(source, target, send, recv, device):
         return pltpu.make_async_remote_copy(
@@ -204,27 +221,34 @@
 
     def own_copy(rel, quarter, rows):
         return remote(
-            eig_ref.at[rows], eig.at[rel, rows], eig_send.at[rel, quarter],
+            eig_ref.at[rows], eig.at[rel, rows], eig_send,
             eig_recv.at[rel, quarter], (flip(band, rel), z),
         )
 
     def forward_copy(rel, quarter, rows):
         return remote(
-            eig.at[rel, rows], eig.at[rel + 1, rows], eig_send.at[rel + 1, quarter],
+            eig.at[rel, rows], eig.at[rel + 1, rows], eig_send,
             eig_recv.at[rel + 1, quarter], (flip(band, 1), z),
         )
 
     def corner_copy(via, quarter, rows):
         return remote(
-            eig.at[via, rows], eig.at[6, rows], eig_send.at[6, quarter],
+            eig.at[via, rows], eig.at[6, rows], eig_send,
             eig_recv.at[6, quarter], (flip(band, 6 - via), z),
         )
 
     def landed(rel, quarter, rows):
         return remote(
-            eig.at[rel, rows], eig.at[rel, rows], eig_send.at[rel, quarter],
+            eig.at[rel, rows], eig.at[rel, rows], eig_send,
             eig_recv.at[rel, quarter], (flip(band, 1), z),
         )
+
+    def z_slot(kind, rel, quarter):
+        if kind == 2:
+            return rel
+        if isinstance(quarter, int) and quarter == N_QUARTER:
+            return n_rel * N_QUARTER + rel
+        return rel * N_QUARTER + quarter
 
     def z_copy(kind, rel, quarter, rows, columns):
         source, target = ((sent, from_edge), (sent, from_mid), (proj, proj))[kind]
@@ -232,7 +256,7 @@
             rows = shifted(rel, rows)
         return remote(
             source.at[rel, rows, columns], target.at[rel, rows, columns],
-            z_send.at[kind, rel, quarter], z_recv.at[kind, rel, quarter],
+            z_send.at[kind // 2], z_recv.at[kind % 2, z_slot(kind, rel, quarter)],
             (band, across if kind == 1 else mate),
         )
 
@@ -325,18 +349,7 @@
     def apply_screen(rel):
         @pl.when(edge)
         def _():
-            for columns, some in ((first_cols, rel < 2), (all_cols, rel >= 2)):
-                @pl.when(some)
-                def _():
-                    for quarter in range(N_QUARTER):
-                        each(
-                            quarter,
-                            lambda rows: z_copy(2, rel, quarter, rows, columns).wait_recv(),
-                        )
-
-            @pl.when(rel < 2)
-            def _():
-                z_copy(2, rel, N_QUARTER, whole_rows, last_cols).wait_recv()
+            z_copy(2, rel, 0, whole_rows, all_cols).wait_recv()
 
         lane = pl.multiple_of(lax.div(lane_of(rel), 128) * 128, 128)
         acc[...] += lax.dot_general(
@@ -428,7 +441,7 @@
         chip_to, z_to = flip(band, 2 * rel), lax.rem(z + k, n_z)
         at = rel * n_z + k - 1
         return remote(
-            fin_out.at[lax.div(chip_to, 2), z_to], fin_in.at[at], fin_send.at[at], fin_recv.at[at],
+            fin_out.at[lax.div(chip_to, 2), z_to], fin_in.at[at], fin_send, fin_recv,
             (chip_to, z_to),
         )
 
@@ -444,47 +457,22 @@
     for swap in swaps:
         swap.wait_send()
 
-    def drain_z(rel, quarter, rows, columns):
-        @pl.when(edge)
-        def _():
-            z_copy(0, rel, quarter, rows, columns).wait_send()
-
-        @pl.when(inner)
-        def _():
-            z_copy(1, rel, quarter, rows, columns).wait_send()
-            z_copy(2, rel, quarter, rows, columns).wait_send()
-
-    def drain(rel, carry):
-        for quarter in range(N_QUARTER):
-            @pl.when(rel > 0)
-            def _():
-                each(quarter, lambda rows: landed(rel, quarter, rows).wait_send())
-
-            @pl.when(rel < 2)
-            def _():
-                each(quarter, lambda rows: drain_z(rel, quarter, rows, first_cols))
-
-            @pl.when(rel >= 2)
-            def _():
-                each(quarter, lambda rows: drain_z(rel, quarter, rows, all_cols))
-
-        @pl.when(rel < 2)
-        def _():
-            drain_z(rel, N_QUARTER, whole_rows, last_cols)
-
-        return carry
-
-    lax.fori_loop(0, n_rel, drain, 0)
+    remote(eig.at[pl.ds(1, n_rel - 1)], eig.at[pl.ds(1, n_rel - 1)], eig_send, eig_recv.at[0, 0], (flip(band, 1), z)).wait_send()
+    remote(sent, sent, z_send.at[0], z_recv.at[0, 0], (band, mate)).wait_send()
+
+    @pl.when(inner)
+    def _():
+        remote(sent, sent, z_send.at[1], z_recv.at[0, 0], (band, mate)).wait_send()
+
     core_copy.wait_send()
 
     total = sig_own[chip, pl.ds(pl.multiple_of(z * fine, fine), fine)]
-    for copy in finals:
-        copy.wait_recv()
+    everything = remote(fin_in, fin_in, fin_send, fin_recv, (band, mate))
+    everything.wait_recv()
     for at in range(fin_in.shape[0]):
         total = total + fin_in[at].astype(jnp.float32)
     out_ref[...] = total
-    for copy in finals:
-        copy.wait_send()
+    everything.wait_send()
 
 
 def per_device(
@@ -499,7 +487,6 @@
     lanes = -(-screening.shape[1] // 128) * 128 + 128
     dma = pltpu.SemaphoreType.DMA
     vmem = pl.BlockSpec(memory_space=pltpu.VMEM)
-    smem = pl.BlockSpec(memory_space=pltpu.SMEM)
     hbm = pl.BlockSpec(memory_space=pl.ANY)
     strip = NB_SIGMA // n_rel
     fine = strip // n_z
@@ -507,9 +494,13 @@
     return pl.pallas_call(
         fused_kernel,
         out_shape=jax.ShapeDtypeStruct((fine, NB_SIGMA), f32),
-        in_specs=[hbm, hbm, hbm, smem, smem, smem, smem],
+        in_specs=[hbm] * 7,
         out_specs=vmem,
         scratch_shapes=[
+            pltpu.SMEM(window_start.shape, jnp.int32),
+            pltpu.SMEM(window_len.shape, jnp.int32),
+            pltpu.SMEM(slot_band.shape, jnp.int32),
+            pltpu.SMEM(occupation.shape, f32),
             pltpu.VMEM((cols, plane_rows), bf16),
             pltpu.VMEM((block, plane_rows), bf16),
             pltpu.VMEM((8, block), f32),
@@ -532,17 +523,17 @@
             pltpu.VMEM((n_rel // 2, strip, NB_SIGMA), f32),
             pltpu.VMEM((n_rel // 2, n_z, fine, NB_SIGMA), bf16),
             pltpu.VMEM((n_rel // 2 * n_z - 1, fine, NB_SIGMA), bf16),
-            dma((4,)),
+            dma((8,)),
             dma((2,)),
             dma((2,)),
+            dma,
             dma((n_rel, N_QUARTER)),
-            dma((n_rel, N_QUARTER)),
-            dma((3, n_rel, N_QUARTER + 1)),
-            dma((3, n_rel, N_QUARTER + 1)),
+            dma((2,)),
+            dma((2, n_rel * N_QUARTER + 2)),
             dma,
             dma,
-            dma((n_rel // 2 * n_z - 1,)),
-            dma((n_rel // 2 * n_z - 1,)),
+            dma,
+            dma,
         ],
         compiler_params=pltpu.CompilerParams(
             collective_id=0, has_side_effects=True, vmem_limit_bytes=60 * 2**20

time: 103 us -> 99.9 us (0.970)
  Pallas kernels: 101 us -> 98.3 us
    pallas_call x1, Pallas kernels: 101 us -> 98.3 us  [per_device(): pl.pallas_call(fused_kernel, out_shape=jax.ShapeDtypeStruct((fine, NB_SIG...]
where the time goes in v4:
time: 99.9 us; the launch traced here: 99.7 us
  Pallas kernels  98.3 us (98%)
  local copies, waits for them, and re-layouts  1.38 us (1%)
    pallas_call x1, Pallas kernels, per_device(): pl.pallas_call(fused_kernel, out_shape=jax.ShapeDtypeStruct((fine, NB_SIG...  98.3 us

profile of v4, /device:TPU:1, one launch (start us, length us, event | category | flops | bytes accessed | tf_op | source)
XLA Modules:
  0.0 99.7 jit_solution(8877647672536799678)
XLA Ops:
  0.0 98.3 %shard_map.73 = f32[16,512]{1,0:T(8,128)} custom-call(bf16[640,2304]{1,0:T(8,128)(2,1)} %bitcast.1, bf16[368,2304]{1,0:T(8,128)(2,1)} %eig_ref.1, bf16[736,2944]{1,0:T(8,128)(2,1)} %screen_ref.1, s32[5]{0:T(128)} %start_hbm.1, s32[5]{0:T(128)} %len_hbm.1, s32[5]{0:T(128)} %slot_hbm.1, f32[16]{0:T(128)} %occ_hbm.1), custom_call_target="tpu_custom_call" | custom-call | tf_op jit(solution)/shard_map/pallas_call | solution.py:494
  98.3 1.4 %copy.9 = f32[16,512]{1,0:T(8,128)} copy(f32[16,512]{1,0:T(8,128)} %shard_map.73) | data formatting | bytes 65536

commit v5 on v4

--- a/solution.py
+++ b/solution.py
@@ -68,13 +68,15 @@
     return top, (value - top.astype(jnp.float32)).astype(jnp.bfloat16)
 
 
-N_QUARTER = 4
-EARLY, PATCH, FULL = 2 * N_QUARTER, 2, 6 * N_QUARTER
+N_PIECE = 5
+EARLY, PATCH, FULL = 2 * N_PIECE, 2, 6 * N_PIECE
 TICKS = EARLY + PATCH + FULL
-LAG_SUM, LAG_TOTAL, LAG_SCREEN = 2, 4, 6
+LAG_SUM, LAG_TOTAL, LAG_SCREEN = 2, 4, 8
 ORDER = (
-    (2, 0), (2, 1), (4, 1), (2, 2), (4, 2), (2, 3), (4, 3), (6, 1), (4, 0), (6, 2), (6, 0), (6, 3),
+    (2, 0), (2, 1), (2, 2), (4, 1), (4, 2), (2, 3), (4, 3), (2, 4), (4, 0), (6, 1), (4, 4), (6, 2),
+    (6, 0), (6, 3), (6, 4),
 )
+Y_FIRST, X_FIRST = (1, 2, 3, 0, 4), (0, 1, 2, 3, 4)
 DONE = tuple(EARLY + rel for rel in range(2)) + tuple(
     EARLY + PATCH + 2 * max(at for at, pair in enumerate(ORDER) if pair[0] == rel) + core
     for rel in (2, 4, 6) for core in range(2)
@@ -90,10 +92,11 @@
     return result
 
 
-def quarter_sizes(depth):
+def piece_sizes(depth):
     units = depth // 16
-    middle = -(-units // N_QUARTER)
-    return 16 * (middle + 1), 16 * middle, 16 * middle, 16 * (units - 3 * middle - 1)
+    middle = -(-units // N_PIECE)
+    rest = units - 3 * middle
+    return 16 * (rest - rest // 2), 16 * middle, 16 * middle, 16 * middle, 16 * (rest // 2)
 
 
 def piece_of(order):
@@ -113,7 +116,7 @@
     mesh_id = pl.DeviceIdType.MESH
     band, z = lax.axis_index("band"), lax.axis_index("pw")
     n_rel, depth, _ = eig.shape
-    sizes = quarter_sizes(depth)
+    sizes = piece_sizes(depth)
     span = proj.shape[1]
     padded = acc.shape[1] // 2
     half_rows = screen_ref.shape[0] // 2
@@ -201,14 +204,14 @@
         if isinstance(quarter, int):
             return sum(sizes[:quarter])
         return pl.multiple_of(
-            quarter * sizes[1] + lax.div(quarter + 3, 4) * (sizes[0] - sizes[1]), 16
+            quarter * sizes[1] + lax.div(quarter + 7, 8) * (sizes[0] - sizes[1]), 16
         )
 
     def each(quarter, act):
         if isinstance(quarter, int):
             act(pl.ds(first_row(quarter), sizes[quarter]))
             return
-        for first, stop in ((0, 1), (1, 3), (3, 4)):
+        for first, stop in ((0, 1), (1, 4), (4, 5)):
             @pl.when((quarter >= first) & (quarter < stop))
             def _():
                 act(pl.ds(first_row(quarter), sizes[first]))
@@ -246,9 +249,9 @@
     def z_slot(kind, rel, quarter):
         if kind == 2:
             return rel
-        if isinstance(quarter, int) and quarter == N_QUARTER:
-            return n_rel * N_QUARTER + rel
-        return rel * N_QUARTER + quarter
+        if isinstance(quarter, int) and quarter == N_PIECE:
+            return n_rel * N_PIECE + rel
+        return rel * N_PIECE + quarter
 
     def z_copy(kind, rel, quarter, rows, columns):
         source, target = ((sent, from_edge), (sent, from_mid), (proj, proj))[kind]
@@ -268,8 +271,8 @@
     ]
     for swap in swaps:
         swap.start()
-    for index in range(N_QUARTER):
-        for rel, quarter in ((1, index), (2, index), (4, (index + 1) % N_QUARTER)):
+    for index in range(N_PIECE):
+        for rel, quarter in ((1, index), (2, X_FIRST[index]), (4, Y_FIRST[index])):
             each(quarter, lambda rows: own_copy(rel, quarter, rows).start())
 
     first_cols, last_cols, all_cols = pl.ds(0, most), pl.ds(most, block), pl.ds(0, cols)
@@ -282,7 +285,7 @@
 
         @pl.when((index >= EARLY) & (index < EARLY + PATCH))
         def _():
-            act(index - EARLY, N_QUARTER, whole_rows, last_cols)
+            act(index - EARLY, N_PIECE, whole_rows, last_cols)
 
         @pl.when((index >= EARLY + PATCH) & (index < TICKS))
         def _():
@@ -313,11 +316,13 @@
             def _():
                 each(quarter, lambda rows: forward_copy(rel, quarter, rows).start())
 
-            @pl.when((rel == 2) & (quarter == 0))
+            outer = (quarter == 0) | (quarter == N_PIECE - 1)
+
+            @pl.when((rel == 2) & outer)
             def _():
-                each(0, lambda rows: corner_copy(2, 0, rows).start())
-
-            @pl.when((rel == 4) & (quarter > 0))
+                each(quarter, lambda rows: corner_copy(2, quarter, rows).start())
+
+            @pl.when((rel == 4) & (quarter > 0) & (quarter < N_PIECE - 1))
             def _():
                 each(quarter, lambda rows: corner_copy(4, quarter, rows).start())
 
@@ -527,9 +532,9 @@
             dma((2,)),
             dma((2,)),
             dma,
-            dma((n_rel, N_QUARTER)),
+            dma((n_rel, N_PIECE)),
             dma((2,)),
-            dma((2, n_rel * N_QUARTER + 2)),
+            dma((2, n_rel * N_PIECE + 2)),
             dma,
             dma,
             dma,

time: 99.9 us -> 99.5 us (level)
  no operation moved by 1% of the time
where the time goes in v5:
time: 99.5 us; the launch traced here: 99.3 us
  Pallas kernels  97.9 us (98%)
  local copies, waits for them, and re-layouts  1.38 us (1%)
    pallas_call x1, Pallas kernels, per_device(): pl.pallas_call(fused_kernel, out_shape=jax.ShapeDtypeStruct((fine, NB_SIG...  97.9 us

profile of v5, /device:TPU:1, one launch (start us, length us, event | category | flops | bytes accessed | tf_op | source)
XLA Modules:
  0.0 99.3 jit_solution(17487207735983666604)
XLA Ops:
  0.0 97.9 %shard_map.73 = f32[16,512]{1,0:T(8,128)} custom-call(bf16[640,2304]{1,0:T(8,128)(2,1)} %bitcast.1, bf16[368,2304]{1,0:T(8,128)(2,1)} %eig_ref.1, bf16[736,2944]{1,0:T(8,128)(2,1)} %screen_ref.1, s32[5]{0:T(128)} %start_hbm.1, s32[5]{0:T(128)} %len_hbm.1, s32[5]{0:T(128)} %slot_hbm.1, f32[16]{0:T(128)} %occ_hbm.1), custom_call_target="tpu_custom_call" | custom-call | tf_op jit(solution)/shard_map/pallas_call | solution.py:499
  97.9 1.4 %copy.9 = f32[16,512]{1,0:T(8,128)} copy(f32[16,512]{1,0:T(8,128)} %shard_map.73) | data formatting | bytes 65536

commit v6 on v5

--- a/solution.py
+++ b/solution.py
@@ -451,7 +451,7 @@
         )
 
     finals = [
-        final_copy(rel, k) for rel in (3, 1, 2, 0) for k in (2, 1, 3, 0) if rel + k > 0
+        final_copy(rel, k) for rel in (3, 2, 1, 0) for k in (2, 1, 3, 0) if rel + k > 0
     ]
     core_copy.wait_recv()
     sig_own[...] += sig_in[...]

time: 99.5 us -> 99.7 us (level)
  no operation moved by 1% of the time
where the time goes in v6:
time: 99.7 us; the launch traced here: 99.5 us
  Pallas kernels  98.1 us (98%)
  local copies, waits for them, and re-layouts  1.38 us (1%)
    pallas_call x1, Pallas kernels, per_device(): pl.pallas_call(fused_kernel, out_shape=jax.ShapeDtypeStruct((fine, NB_SIG...  98.1 us

profile of v6, /device:TPU:1, one launch (start us, length us, event | category | flops | bytes accessed | tf_op | source)
XLA Modules:
  0.0 99.5 jit_solution(14906694156188041713)
XLA Ops:
  0.0 98.1 %shard_map.73 = f32[16,512]{1,0:T(8,128)} custom-call(bf16[640,2304]{1,0:T(8,128)(2,1)} %bitcast.1, bf16[368,2304]{1,0:T(8,128)(2,1)} %eig_ref.1, bf16[736,2944]{1,0:T(8,128)(2,1)} %screen_ref.1, s32[5]{0:T(128)} %start_hbm.1, s32[5]{0:T(128)} %len_hbm.1, s32[5]{0:T(128)} %slot_hbm.1, f32[16]{0:T(128)} %occ_hbm.1), custom_call_target="tpu_custom_call" | custom-call | tf_op jit(solution)/shard_map/pallas_call | solution.py:499
  98.1 1.4 %copy.9 = f32[16,512]{1,0:T(8,128)} copy(f32[16,512]{1,0:T(8,128)} %shard_map.73) | data formatting | bytes 65536
